TPU v7x, 128 devices: a whole 4x4x4 slice. The times are simulated.
128 devices in a mesh: rows: 16 (over x, y), cols: 8 (over z, core).
Axes of the slice: x: 4, y: 4, z: 4, core: 2. Of those that a mesh axis runs over, the one named last changes fastest.
Arguments:
- coarse: float32 [1024, 1024], P('rows', 'cols'), may hold values from -6 to 6
- detail4: float32 [3, 1024, 1024], P(None, 'rows', 'cols'), may hold values from -6 to 6
- detail3: float32 [3, 2048, 2048], P(None, 'rows', 'cols'), may hold values from -6 to 6
- detail2: float32 [3, 4096, 4096], P(None, 'rows', 'cols'), may hold values from -6 to 6
- detail1: float32 [3, 8192, 8192], P(None, 'rows', 'cols'), may hold values from -6 to 6
Outputs:
- image: float32 [16384, 16384], P('rows', 'cols')
All inputs are finite; a program needn't handle non-finite values.
Results may differ from a plain program's by a relative error of at most 0.00013.
Values sent between devices are 32-bit elements; how exact they have to be, the bound alone decides.
A program may use at most 128 MiB of HBM per device.

v0:
```python
import functools

import jax
import jax.numpy as jnp
from jax import lax
from jax.experimental import pallas as pl
from jax.experimental.pallas import tpu as pltpu
from jax.sharding import PartitionSpec as P

ALPHA = -1.586134342059924
BETA = -0.052980118572961
GAMMA = 0.882911075530934
DELTA = 0.443506852043971
SCALE = 1.149604398860241
UP2 = SCALE * SCALE
DOWN2 = 1.0 / (SCALE * SCALE)

B = 128
HALO = 8
F32 = jnp.float32
MESH = pl.DeviceIdType.MESH

DIRS = ((-1, 0), (1, 0), (0, -1), (0, 1), (-1, -1), (-1, 1), (1, -1), (1, 1))


def iota(axis):
    return lax.broadcasted_iota(jnp.int32, (8, B), axis)


def turn(x, amount):
    amount = amount % B
    return x if amount == 0 else pltpu.roll(x, amount, axis=1)


def row_blocks(level):
    return -(-level[2] // B)


def depth_of(levels, k):
    return 2 if k == len(levels) - 1 else 4


def row_plan(levels):
    plan, at = [], 0
    for k, (arrays, blocks, h) in enumerate(levels):
        for a in range(arrays):
            for b in range(blocks):
                plan.append((k, a, b, at))
                at += depth_of(levels, k)
    return plan, -(-at // 8) * 8


def column_plan(levels):
    plan, at = [], 0
    for k, level in enumerate(levels):
        for a in range(level[0]):
            for n in range(row_blocks(level)):
                plan.append((k, a, n, at))
                at += depth_of(levels, k)
    return plan, -(-at // 8) * 8


def stack_offsets(levels):
    offsets, at = [], 0
    for _, blocks, _ in levels:
        offsets.append(at)
        at += 8 * blocks
    return offsets


def lift_rows(count, s, r, dst):
    run = (count + 8) // 8

    def rows(ref, t):
        return ref[pl.ds(HALO - 4 + t, 8, stride=run), :]

    r0, s1, r1, s2 = {}, {}, {}, {}
    for t in range(-2, run + 2):
        r0[t] = rows(r, t)
        if t < -1:
            continue
        s1[t] = rows(s, t) - DELTA * (r0[t] + r0[t - 1])
        if t < 0:
            continue
        r1[t - 1] = r0[t - 1] - GAMMA * (s1[t - 1] + s1[t])
        if t < 1:
            continue
        n = t - 1
        s2[n] = s1[n] - BETA * (r1[n] + r1[n - 1])
        if n < run:
            dst[pl.ds(2 * n, 8, stride=2 * run), :] = s2[n]
        if n >= 1:
            dst[pl.ds(2 * n - 1, 8, stride=2 * run), :] = r1[n - 1] - ALPHA * (s2[n - 1] + s2[n])


def scaled(x, scale):
    return x if scale is None else x * scale


def turn_back(level, final, n, lifted, edge, dst):
    _, blocks, h = level
    count = min(B, h)
    at = pl.ds(HALO + n * B, count)
    for j in range(2 * blocks):
        dst[j, at, :] = lifted[pl.ds(HALO + j * B, B), :].T[:count]
    if not final:
        edge[0:8, :] = lifted[pl.ds(HALO + 2 * blocks * B, 8), :]
        edge[B - 8 : B, :] = lifted[0:8, :]
        dst[2 * blocks, at, :] = edge[...].T[:count]


def halo_transpose(levels, hn, cn, scale, dst):
    group = iota(1) // 8
    offsets = stack_offsets(levels)
    first = last = None
    for off, (_, blocks, _) in zip(offsets, levels):
        f, l = group == off // 8, group == off // 8 + blocks - 1
        first = f if first is None else first | f
        last = l if last is None else last | l
    t = scaled(hn[...].T, scale)
    ct = scaled(cn[...].T, scale)
    dst[pl.ds(HALO, B), :] = t
    dst[pl.ds(0, 8), :] = jnp.where(first, ct[B - 8 :], turn(t[B - 8 :], 8))
    dst[pl.ds(HALO + B, 8), :] = jnp.where(last, ct[:8], turn(t[:8], -8))


def halo_back(levels, which, lifted, edge, dsts):
    low = iota(1) < 64
    offsets = stack_offsets(levels)
    for j in range(2):
        y = lifted[pl.ds(HALO + j * B, B), :].T
        for k in which:
            _, blocks, h = levels[k]
            for b in range(blocks):
                tile = y[offsets[k] + 8 * b : offsets[k] + 8 * b + 8]
                dsts[k][2 * b + j, pl.ds(0, 8), :] = tile
                dsts[k][2 * b + j, pl.ds(HALO + h, 8), :] = tile
    which = [k for k in which if k < len(levels) - 1]
    if which:
        edge[0:8, :] = lifted[pl.ds(HALO + 2 * B, 8), :]
        edge[B - 8 : B, :] = lifted[0:8, :]
        y = edge[...].T
        for k in which:
            _, blocks, h = levels[k]
            end = offsets[k] + 8 * (blocks - 1)
            tile = jnp.where(low, y[end : end + 8], y[offsets[k] : offsets[k] + 8])
            dsts[k][2 * blocks, pl.ds(0, 8), :] = tile
            dsts[k][2 * blocks, pl.ds(HALO + h, 8), :] = tile


def exchange_kernel(levels, *refs):
    coarse, d4, d3, d2, d1 = refs[:5]
    ws, zs = refs[5:9], refs[9:13]
    zh, c4, ch = refs[13:16]
    ns, xs = refs[16:20], refs[20:24]
    (hn, cn, sh, rh, hd, lifted, edge, rows_out, cols_out, corners_out, rows_in, cols_in, corners_in,
     load_sem, send_sem, recv_sem) = refs[24:]
    nr, nc = lax.axis_size("rows"), lax.axis_size("cols")
    r, c = lax.axis_index("rows"), lax.axis_index("cols")
    top = len(levels) - 1

    def neighbour(step):
        return (lax.rem(r + step[0] + nr, nr), lax.rem(c + step[1] + nc, nc))

    barrier = pltpu.get_barrier_semaphore()
    for step in DIRS:
        pl.semaphore_signal(barrier, inc=1, device_id=neighbour(step), device_id_type=MESH)

    loads = []

    def load(src, dst):
        copy = pltpu.make_async_copy(src, dst, load_sem.at[len(loads)])
        copy.start()
        loads.append(copy)

    h = levels[0][2]
    load(coarse, ns[0].at[3, pl.ds(0, h), :])
    load(d4, ns[0].at[pl.ds(0, 3), pl.ds(0, h), :])
    load(d3, ns[1])
    load(d2, ns[2])
    _, blocks, h = levels[top]
    w = blocks * B
    for at in (pl.ds(0, 8), pl.ds(h - 8, 8)):
        load(d1.at[:, at, :], ns[top].at[:, at, :])
    inner = pl.ds(8, h - 16)
    for at in (pl.ds(0, B), pl.ds(w - B, B)):
        load(d1.at[:, inner, at], ns[top].at[:, inner, at])
    for a in range(3):
        at = pl.ds(B, w - 2 * B)
        load(d1.at[a, inner, at], ns[top].at[a, inner, at])

    def columns_of(k, a):
        return c4 if a == 3 else zs[k] if a == 0 else xs[k].at[a - 1]

    def transpose(k, a, n, b):
        scale = (None, None, DOWN2, UP2)[a]
        columns_of(k, a)[n, pl.ds(HALO + b * B, B), :] = scaled(
            ns[k][a, pl.ds(n * B, B), pl.ds(b * B, B)].T, scale)

    for copy in loads[:4]:
        copy.wait()
    for k in range(top):
        for a in range(levels[k][0]):
            for n in range(row_blocks(levels[k])):
                for b in range(levels[k][1]):
                    transpose(k, a, n, b)
    for copy in loads[4:8]:
        copy.wait()
    for a in range(3):
        for n in range(row_blocks(levels[top])):
            for b in (0, levels[top][1] - 1):
                transpose(top, a, n, b)

    rows, _ = row_plan(levels)
    for k, a, b, at in rows:
        depth, h = depth_of(levels, k), levels[k][2]
        here = pl.ds(b * B, B)
        rows_out[0, pl.ds(at, depth), :] = ns[k][a, pl.ds(0, depth), here]
        rows_out[1, pl.ds(at, depth), :] = ns[k][a, pl.ds(h - depth, depth), here]
    group = iota(1) // 4
    arrays = [(k, a) for k in range(top + 1) for a in range(levels[k][0])]
    for d in range(4):
        step = DIRS[4 + d]
        packed = jnp.zeros((8, B), F32)
        for q, (k, a) in enumerate(arrays):
            _, blocks, h = levels[k]
            at = pl.ds(0 if step[0] < 0 else h - 8, 8)
            if step[1] < 0:
                packed = jnp.where(group == q, turn(ns[k][a, at, pl.ds(0, B)], 4 * q), packed)
            else:
                packed = jnp.where(
                    group == 31 - q, turn(ns[k][a, at, pl.ds((blocks - 1) * B, B)], -4 * q), packed)
        corners_out[d] = packed
    columns, _ = column_plan(levels)
    for k, a, n, at in columns:
        depth, w = depth_of(levels, k), levels[k][1] * B
        cols_out[0, pl.ds(at, depth), :] = columns_of(k, a)[n, pl.ds(HALO, depth), :]
        cols_out[1, pl.ds(at, depth), :] = columns_of(k, a)[n, pl.ds(HALO + w - depth, depth), :]

    pl.semaphore_wait(barrier, len(DIRS))
    sends = []
    for d, step in enumerate(DIRS):
        if d < 2:
            src, dst = rows_out.at[d], rows_in.at[d]
        elif d < 4:
            src, dst = cols_out.at[d - 2], cols_in.at[d - 2]
        else:
            src, dst = corners_out.at[d - 4], corners_in.at[d - 4]
        sends.append(pltpu.make_async_remote_copy(
            src_ref=src, dst_ref=dst, send_sem=send_sem.at[d], recv_sem=recv_sem.at[d],
            device_id=neighbour(step), device_id_type=MESH))
    for d in (4, 5, 6, 7, 0, 1, 2, 3):
        sends[d].start()

    for copy in loads[8:]:
        copy.wait()

    def middle(a, carry):
        for n in range(row_blocks(levels[top])):
            for b in range(1, levels[top][1] - 1):
                at = pl.ds(HALO + b * B, B)
                block = ns[top][a, pl.ds(n * B, B), pl.ds(b * B, B)].T
                xs[top][a - 1, n, at, :] = block * jnp.where(a == 2, F32(DOWN2), F32(1.0))
        return carry

    for n in range(row_blocks(levels[top])):
        for b in range(1, levels[top][1] - 1):
            transpose(top, 0, n, b)
    lax.fori_loop(1, 3, middle, 0)

    sends[2].wait()
    sends[3].wait()
    for k, a, n, at in columns:
        depth, w = depth_of(levels, k), levels[k][1] * B
        columns_of(k, a)[n, pl.ds(HALO + w, depth), :] = cols_in[0, pl.ds(at, depth), :]
        columns_of(k, a)[n, pl.ds(HALO - depth, depth), :] = cols_in[1, pl.ds(at, depth), :]
    for k in (3, 2, 1, 0):
        for n in range(row_blocks(levels[k])):
            part = lifted.at[n, pl.ds(0, 2 * levels[k][1] * B + 16), :]
            lift_rows(levels[k][1] * B, xs[k].at[0, n], xs[k].at[1, n], part)
            turn_back(levels[k], k == top, n, part, edge, ws[k])

    for d in (0, 1, 4, 5, 6, 7):
        sends[d].wait()
    offsets = stack_offsets(levels)
    for k, a, b, at in rows:
        depth, base = depth_of(levels, k), offsets[k] + 8 * b
        hn[a, pl.ds(base, depth), :] = rows_in[0, pl.ds(at, depth), :]
        hn[a, pl.ds(base + 8 - depth, depth), :] = rows_in[1, pl.ds(at, depth), :]
    low, bottom = iota(1) < 64, iota(0) < 4
    for q, (k, a) in enumerate(arrays):
        tile = jnp.where(
            bottom,
            jnp.where(low, turn(corners_in[0], -4 * q), turn(corners_in[1], 4 * q)),
            jnp.where(low, turn(corners_in[2], -4 * q), turn(corners_in[3], 4 * q)))
        cn[a, pl.ds(offsets[k], 8), :] = tile
        cn[a, pl.ds(offsets[k] + 8 * (levels[k][1] - 1), 8), :] = tile
    halo_transpose(levels, hn.at[1], cn.at[1], None, sh)
    halo_transpose(levels, hn.at[2], cn.at[2], DOWN2, rh)
    halo_transpose(levels, hn.at[0], cn.at[0], None, zh)
    halo_transpose(levels, hn.at[3], cn.at[3], UP2, ch)
    lift_rows(B, sh, rh, hd)
    halo_back(levels, range(top + 1), hd, edge, ws)


def synthesis_kernel(levels, *refs):
    ws, zs = refs[:4], refs[4:8]
    zh, c4, ch = refs[8:11]
    out = refs[11]
    lows = (None,) + refs[12:15]
    image = refs[15]
    us, ts = refs[16:20], (c4,) + refs[20:23]
    hn, cn, th, hd, lifted, edge, out_sem = refs[23:]
    top = len(levels) - 1
    offsets = stack_offsets(levels)
    bottom = iota(0) < 4

    for k, level in enumerate(levels):
        _, blocks, h = level
        w = blocks * B
        final = k == top
        n_rows = row_blocks(level)
        if k == 0:
            halo = ch
        else:
            halo = th
            low = lows[k]
            for b in range(blocks + 1):
                tile = jnp.where(bottom, low[b, pl.ds(HALO + h, 8), :], low[b, pl.ds(0, 8), :])
                if b < blocks:
                    hn[pl.ds(offsets[k] + 8 * b, 8), :] = tile
                else:
                    cn[pl.ds(offsets[k], 8), :] = tile
                    cn[pl.ds(offsets[k] + 8 * (blocks - 1), 8), :] = tile
            halo_transpose(levels, hn, cn, UP2, th)
            for n in range(n_rows):
                at = pl.ds(HALO + n * B, B)
                for b in range(blocks):
                    ts[k][n, pl.ds(HALO + b * B, B), :] = low[b, at, :].T * UP2
                side = low[blocks, at, :].T * UP2
                ts[k][n, pl.ds(0, 8), :] = side[B - 8 :]
                ts[k][n, pl.ds(HALO + w, 8), :] = side[:8]
        lift_rows(B, halo, zh, hd)
        halo_back(levels, (k,), hd, edge, {k: us[k]})
        for n in range(n_rows):
            part = lifted.at[n, pl.ds(0, 2 * w + 16), :]
            lift_rows(w, ts[k].at[n], zs[k].at[n], part)
            turn_back(level, final, n, part, edge, us[k])
        if not final:
            for j in range(2 * blocks + 1):
                lift_rows(h, us[k].at[j], ws[k].at[j], lows[k + 1].at[j])
        else:
            def body(j, carry, h=h):
                lift_rows(h, us[top].at[j], ws[top].at[j], image.at[j])
                pltpu.make_async_copy(
                    image.at[j, pl.ds(HALO, 2 * h), :],
                    out.at[:, pl.ds(pl.multiple_of(j * B, B), B)], out_sem.at[j]).start()
                return carry

            lax.fori_loop(0, 2 * blocks, body, 0)
            for j in range(2 * blocks):
                pltpu.make_async_copy(
                    image.at[j, pl.ds(HALO, 2 * h), :], out.at[:, pl.ds(j * B, B)], out_sem.at[j]).wait()


def per_device(coarse, d4, d3, d2, d1):
    levels = []
    for k, x in enumerate((d4, d3, d2, d1)):
        levels.append((4 if k == 0 else 3, x.shape[2] // B, x.shape[1]))
    levels = tuple(levels)
    top = len(levels) - 1
    _, row_count = row_plan(levels)
    _, col_count = column_plan(levels)
    hbm = pl.BlockSpec(memory_space=pltpu.HBM)
    vmem = pl.BlockSpec(memory_space=pltpu.VMEM)
    wide = [2 * b + (0 if k == top else 1) for k, (_, b, _) in enumerate(levels)]
    across = [(row_blocks(l), l[1] * B + 2 * HALO, B) for l in levels]
    strips = [(n, l[2] + 2 * HALO, B) for n, l in zip(wide, levels)]
    stack = (B + 2 * HALO, B)
    lifted = pltpu.VMEM((across[top][0], 2 * levels[top][1] * B + 2 * HALO, B), F32)
    between = pl.pallas_call(
        functools.partial(exchange_kernel, levels),
        out_shape=[pltpu.VMEM(s, F32) for s in strips + across + [stack, across[0], stack]],
        in_specs=[hbm] * 5,
        out_specs=[vmem] * 11,
        scratch_shapes=[
            *[pltpu.VMEM((a, max(B, h), b * B), F32) for a, b, h in levels],
            *[pltpu.VMEM((2,) + s, F32) for s in across],
            pltpu.VMEM((4, B, B), F32),
            pltpu.VMEM((4, B, B), F32),
            pltpu.VMEM(stack, F32),
            pltpu.VMEM(stack, F32),
            pltpu.VMEM((2 * B + 2 * HALO, B), F32),
            lifted,
            pltpu.VMEM((B, B), F32),
            pltpu.VMEM((2, row_count, B), F32),
            pltpu.VMEM((2, col_count, B), F32),
            pltpu.VMEM((4, 8, B), F32),
            pltpu.VMEM((2, row_count, B), F32),
            pltpu.VMEM((2, col_count, B), F32),
            pltpu.VMEM((4, 8, B), F32),
            pltpu.SemaphoreType.DMA((11,)),
            pltpu.SemaphoreType.DMA((8,)),
            pltpu.SemaphoreType.DMA((8,)),
        ],
        compiler_params=pltpu.CompilerParams(
            collective_id=0, has_side_effects=True, vmem_limit_bytes=26 * 2**20),
    )(*[pltpu.with_memory_space_constraint(x, pltpu.HBM) for x in (coarse, d4, d3, d2, d1)])
    blocks, h = levels[top][1], levels[top][2]
    return pl.pallas_call(
        functools.partial(synthesis_kernel, levels),
        out_shape=jax.ShapeDtypeStruct((2 * h, 2 * blocks * B), F32),
        in_specs=[vmem] * 11,
        out_specs=pl.BlockSpec(memory_space=pl.ANY),
        scratch_shapes=[
            *[pltpu.VMEM((levels[k][1] + 1, levels[k][2] + 2 * HALO, B), F32) for k in (1, 2, 3)],
            pltpu.VMEM((2 * blocks, 2 * h + 2 * HALO, B), F32),
            *[pltpu.VMEM(s, F32) for s in strips],
            *[pltpu.VMEM(s, F32) for s in across[1:]],
            pltpu.VMEM((B, B), F32),
            pltpu.VMEM((B, B), F32),
            pltpu.VMEM(stack, F32),
            pltpu.VMEM((2 * B + 2 * HALO, B), F32),
            lifted,
            pltpu.VMEM((B, B), F32),
            pltpu.SemaphoreType.DMA((2 * blocks,)),
        ],
        compiler_params=pltpu.CompilerParams(vmem_limit_bytes=28 * 2**20),
    )(*between)


def solution(mesh):
    return jax.shard_map(
        per_device,
        mesh=mesh,
        in_specs=(
            P("rows", "cols"),
            P(None, "rows", "cols"),
            P(None, "rows", "cols"),
            P(None, "rows", "cols"),
            P(None, "rows", "cols"),
        ),
        out_specs=P("rows", "cols"),
        check_vma=False,
    )
```

profile of v0, /device:TPU:0, one launch (start us, length us, event | category | flops | bytes accessed | tf_op | source)
XLA Modules:
  0.0 21.8 jit_solution(13740117903687044408)
XLA Ops:
  0.0 13.8 %shard_map.55 = (f32[3,80,128]{2,1,0:T(8,128)S(1)}, f32[5,144,128]{2,1,0:T(8,128)S(1)}, f32[9,272,128]{2,1,0:T(8,128)S(1)}, f32[16,528,128]{2,1,0:T(8,128)S(1)},...) custom-call(f32[64,128]{1,0:T(8,128)} %refs_0_.1, ...), custom_call_target="tpu_custom_call" | custom-call | tf_op jit(solution)/shard_map/pallas_call | solution.py:381
  13.8 8.0 %shard_map.56 = f32[1024,2048]{1,0:T(8,128)} custom-call(f32[3,80,128]{2,1,0:T(8,128)S(1)} %get-tuple-element.16.refs_0_, f32[5,144,128]{2,1,0:T(8,128)S(1)} %get-tuple-element.17.refs_1_, f32[9,272,128]{2,1,0:T(8,128)S(1)} %get-tuple-element.18.refs_2_, f32[16,528,128]{2,1,0:T(8,128)S(1)} %get-tuple-element.19.refs_3_, ...), custom_call_target="tpu_custom_call" | custom-call | tf_op jit(solution)/shard_map/pallas_call | solution.py:410
where the time goes:
time: 21.9 us; the launch traced here: 21.8 us
  Pallas kernels  21.8 us (100%)
    pallas_call x1, Pallas kernels, per_device(): pl.pallas_call(functools.partial(exchange_kernel, levels), out_shape=[plt...  13.8 us
    pallas_call x1, Pallas kernels, per_device(): pl.pallas_call(functools.partial(synthesis_kernel, levels), out_shape=jax...  7.95 us

commit v1 on v0

--- a/solution.py
+++ b/solution.py
@@ -69,10 +69,13 @@
 
 
 def lift_rows(count, s, r, dst):
-    run = (count + 8) // 8
-
+    lift_runs((count + 8) // 8, s, HALO - 4, r, HALO - 4, dst)
+
+
+def lift_runs(run, s, s_at, r, r_at, dst):
     def rows(ref, t):
-        return ref[pl.ds(HALO - 4 + t, 8, stride=run), :]
+        at = s_at if ref is s else r_at
+        return ref[pl.ds(at + t, 8, stride=run), :]
 
     r0, s1, r1, s2 = {}, {}, {}, {}
     for t in range(-2, run + 2):
@@ -148,13 +151,50 @@
             dsts[k][2 * blocks, pl.ds(HALO + h, 8), :] = tile
 
 
+def strip_rows(k):
+    return (16, 16, 24, 40)[k]
+
+
+def strip_sides(levels, k, main, ct, dst):
+    _, blocks, h = levels[k]
+    keep, off = strip_rows(k), stack_offsets(levels)[k]
+    lane = iota(1)
+    n = row_blocks(levels[k])
+    start = h - keep - B * (n - 1)
+    w = blocks * B
+    for at, corner, shift in ((0, ct[B - 8 :], off), (HALO + w, ct[:8], off + 8 * (blocks - 1))):
+        here = pl.ds(at, 8)
+        dst[here, :] = jnp.where(
+            lane < 8, turn(corner, -shift),
+            jnp.where(
+                lane < 8 + keep, turn(main[0, here, :], 8),
+                jnp.where(lane < 8 + 2 * keep, turn(main[n - 1, here, :], 8 + keep - start),
+                          turn(corner, 8 + 2 * keep - shift))))
+
+
+def at_of(levels, k, a, b):
+    return b if a == 3 else 1 + sum(l[1] for l in levels[:k]) + b
+
+
+def columns_from(level, low, dst):
+    _, blocks, _ = level
+    for n in range(row_blocks(level)):
+        at = pl.ds(HALO + n * B, B)
+        for b in range(blocks):
+            dst[n, pl.ds(HALO + b * B, B), :] = low[b, at, :].T * UP2
+        side = low[blocks, at, :].T * UP2
+        dst[n, pl.ds(0, 8), :] = side[B - 8 :]
+        dst[n, pl.ds(HALO + blocks * B, 8), :] = side[:8]
+
+
 def exchange_kernel(levels, *refs):
     coarse, d4, d3, d2, d1 = refs[:5]
-    ws, zs = refs[5:9], refs[9:13]
-    zh, c4, ch = refs[13:16]
-    ns, xs = refs[16:20], refs[20:24]
-    (hn, cn, sh, rh, hd, lifted, edge, rows_out, cols_out, corners_out, rows_in, cols_in, corners_in,
-     load_sem, send_sem, recv_sem) = refs[24:]
+    ws, zts, ct_out, image = refs[5:9], refs[9:13], refs[13], refs[14]
+    ns, xs, zs, us = refs[15:19], refs[19:23], refs[23:27], refs[27:31]
+    lows, ts = (None,) + refs[31:34], refs[34:38]
+    c4 = ts[0]
+    (hn, cn, sh, rh, hd, lifted, edge, ds, rows_out, cols_out, corners_out, rows_in, cols_in, corners_in,
+     load_sem, send_sem, recv_sem) = refs[38:]
     nr, nc = lax.axis_size("rows"), lax.axis_size("cols")
     r, c = lax.axis_index("rows"), lax.axis_index("cols")
     top = len(levels) - 1
@@ -280,6 +320,33 @@
             lift_rows(levels[k][1] * B, xs[k].at[0, n], xs[k].at[1, n], part)
             turn_back(levels[k], k == top, n, part, edge, ws[k])
 
+    for k, level in enumerate(levels):
+        _, blocks, h = level
+        w = blocks * B
+        if k > 0:
+            columns_from(level, lows[k], ts[k])
+        for n in range(row_blocks(level)):
+            part = lifted.at[n, pl.ds(0, 2 * w + 16), :]
+            lift_rows(w, ts[k].at[n], zs[k].at[n], part)
+            turn_back(level, k == top, n, part, edge, us[k])
+        if k < top:
+            for j in range(2 * blocks + 1):
+                lift_rows(h, us[k].at[j], ws[k].at[j], lows[k + 1].at[j])
+        else:
+            def body(j, carry, h=h):
+                lift_rows(h, us[top].at[j], ws[top].at[j], image.at[j])
+                return carry
+
+            lax.fori_loop(0, 2 * blocks, body, 0)
+
+    for k, (_, blocks, h) in enumerate(levels):
+        keep = strip_rows(k)
+        for a in (0, 3) if k == 0 else (0,):
+            for b in range(blocks):
+                at = pl.ds(b * B, B)
+                ds[at_of(levels, k, a, b), pl.ds(8, keep), :] = ns[k][a, pl.ds(0, keep), at]
+                ds[at_of(levels, k, a, b), pl.ds(8 + keep, keep), :] = ns[k][a, pl.ds(h - keep, keep), at]
+
     for d in (0, 1, 4, 5, 6, 7):
         sends[d].wait()
     offsets = stack_offsets(levels)
@@ -297,70 +364,103 @@
         cn[a, pl.ds(offsets[k] + 8 * (levels[k][1] - 1), 8), :] = tile
     halo_transpose(levels, hn.at[1], cn.at[1], None, sh)
     halo_transpose(levels, hn.at[2], cn.at[2], DOWN2, rh)
-    halo_transpose(levels, hn.at[0], cn.at[0], None, zh)
-    halo_transpose(levels, hn.at[3], cn.at[3], UP2, ch)
+    for k, a, b, at in rows:
+        if a in (0, 3):
+            depth, keep = depth_of(levels, k), strip_rows(k)
+            strip = at_of(levels, k, a, b)
+            ds[strip, pl.ds(8 + 2 * keep, depth), :] = rows_in[0, pl.ds(at, depth), :]
+            ds[strip, pl.ds(8 - depth, depth), :] = rows_in[1, pl.ds(at, depth), :]
+            (ct_out if a == 3 else zts[k])[pl.ds(HALO + b * B, B), :] = scaled(
+                ds[strip].T, UP2 if a == 3 else None)
+    side = cn[0].T
+    for k in range(top + 1):
+        strip_sides(levels, k, zs[k], side, zts[k])
+    strip_sides(levels, 0, c4, cn[3].T * UP2, ct_out)
     lift_rows(B, sh, rh, hd)
     halo_back(levels, range(top + 1), hd, edge, ws)
 
 
-def synthesis_kernel(levels, *refs):
-    ws, zs = refs[:4], refs[4:8]
-    zh, c4, ch = refs[8:11]
-    out = refs[11]
-    lows = (None,) + refs[12:15]
-    image = refs[15]
-    us, ts = refs[16:20], (c4,) + refs[20:23]
-    hn, cn, th, hd, lifted, edge, out_sem = refs[23:]
+def strip_kernel(levels, *refs):
+    ws, zts, ct, image = refs[:4], refs[4:8], refs[8], refs[9]
+    out = refs[10]
+    lows = (None,) + refs[11:14]
+    ends, us, lifted, edge, th, out_sem, end_sem = refs[14:]
     top = len(levels) - 1
-    offsets = stack_offsets(levels)
-    bottom = iota(0) < 4
+    _, blocks, h = levels[top]
+    rows = 2 * h
+    cut = 64
+
+    def main(j, start):
+        at = pl.ds(cut, rows - 2 * cut)
+        return pltpu.make_async_copy(
+            image.at[j, pl.ds(HALO + cut, rows - 2 * cut), :], out.at[at, pl.ds(start, B)], out_sem.at[j])
+
+    def send(j, carry):
+        main(j, pl.multiple_of(j * B, B)).start()
+        return carry
+
+    lax.fori_loop(0, 2 * blocks, send, 0)
 
     for k, level in enumerate(levels):
-        _, blocks, h = level
-        w = blocks * B
+        _, nb, h = level
+        w = nb * B
         final = k == top
-        n_rows = row_blocks(level)
+        keep = strip_rows(k)
+        size = 2 * keep + 16
         if k == 0:
-            halo = ch
+            t = ct
         else:
-            halo = th
-            low = lows[k]
-            for b in range(blocks + 1):
-                tile = jnp.where(bottom, low[b, pl.ds(HALO + h, 8), :], low[b, pl.ds(0, 8), :])
-                if b < blocks:
-                    hn[pl.ds(offsets[k] + 8 * b, 8), :] = tile
-                else:
-                    cn[pl.ds(offsets[k], 8), :] = tile
-                    cn[pl.ds(offsets[k] + 8 * (blocks - 1), 8), :] = tile
-            halo_transpose(levels, hn, cn, UP2, th)
-            for n in range(n_rows):
-                at = pl.ds(HALO + n * B, B)
-                for b in range(blocks):
-                    ts[k][n, pl.ds(HALO + b * B, B), :] = low[b, at, :].T * UP2
-                side = low[blocks, at, :].T * UP2
-                ts[k][n, pl.ds(0, 8), :] = side[B - 8 :]
-                ts[k][n, pl.ds(HALO + w, 8), :] = side[:8]
-        lift_rows(B, halo, zh, hd)
-        halo_back(levels, (k,), hd, edge, {k: us[k]})
-        for n in range(n_rows):
-            part = lifted.at[n, pl.ds(0, 2 * w + 16), :]
-            lift_rows(w, ts[k].at[n], zs[k].at[n], part)
-            turn_back(level, final, n, part, edge, us[k])
+            t = th
+            for b in range(nb):
+                t[pl.ds(HALO + b * B, B), :] = lows[k][b].T * UP2
+            side = lows[k][nb].T * UP2
+            t[pl.ds(0, 8), :] = side[B - 8 :]
+            t[pl.ds(HALO + w, 8), :] = side[:8]
+        part = lifted.at[pl.ds(0, 2 * w + 16), :]
+        lift_rows(w, t, zts[k], part)
+        for j in range(2 * nb):
+            us[j] = lifted[pl.ds(HALO + j * B, B), :].T
         if not final:
-            for j in range(2 * blocks + 1):
-                lift_rows(h, us[k].at[j], ws[k].at[j], lows[k + 1].at[j])
+            edge[0:8, :] = lifted[pl.ds(HALO + 2 * w, 8), :]
+            edge[B - 8 : B, :] = lifted[0:8, :]
+            us[2 * nb] = edge[...].T
+        run = keep // 8
+
+        def strips(j, first, second, level=level, k=k):
+            _, _, h = level
+            keep = strip_rows(k)
+            run = keep // 8
+            lift_runs(run, us.at[j], 4, ws[k].at[j], 4, first)
+            lift_runs(run, us.at[j], 8 + 2 * keep + 4 - 8 * run, ws[k].at[j], HALO + h + 4 - 8 * run, second)
+
+        if not final:
+            following = strip_rows(k + 1)
+            made = 16 * run
+            for j in range(2 * nb + 1):
+                strips(j, ends.at[0, j, pl.ds(0, made), :], ends.at[1, j, pl.ds(0, made), :])
+                lows[k + 1][j, pl.ds(0, 8 + following), :] = ends[0, j, pl.ds(0, 8 + following), :]
+                lows[k + 1][j, pl.ds(8 + following, 8 + following), :] = ends[
+                    1, j, pl.ds(made - 8 - following, 8 + following), :]
         else:
-            def body(j, carry, h=h):
-                lift_rows(h, us[top].at[j], ws[top].at[j], image.at[j])
-                pltpu.make_async_copy(
-                    image.at[j, pl.ds(HALO, 2 * h), :],
-                    out.at[:, pl.ds(pl.multiple_of(j * B, B), B)], out_sem.at[j]).start()
+            made = 16 * run
+
+            def end(j, side, start):
+                row = (HALO, made - 8 - cut)[side]
+                return pltpu.make_async_copy(
+                    ends.at[side, j, pl.ds(row, cut), :],
+                    out.at[pl.ds((0, rows - cut)[side], cut), pl.ds(start, B)], end_sem.at[side, j])
+
+            def body(j, carry):
+                strips(j, ends.at[0, j, pl.ds(0, made), :], ends.at[1, j, pl.ds(0, made), :])
+                for side in range(2):
+                    end(j, side, pl.multiple_of(j * B, B)).start()
                 return carry
 
-            lax.fori_loop(0, 2 * blocks, body, 0)
-            for j in range(2 * blocks):
-                pltpu.make_async_copy(
-                    image.at[j, pl.ds(HALO, 2 * h), :], out.at[:, pl.ds(j * B, B)], out_sem.at[j]).wait()
+            lax.fori_loop(0, 2 * nb, body, 0)
+            for j in range(2 * nb):
+                main(j, j * B).wait()
+                for side in range(2):
+                    end(j, side, j * B).wait()
 
 
 def per_device(coarse, d4, d3, d2, d1):
@@ -377,22 +477,30 @@
     across = [(row_blocks(l), l[1] * B + 2 * HALO, B) for l in levels]
     strips = [(n, l[2] + 2 * HALO, B) for n, l in zip(wide, levels)]
     stack = (B + 2 * HALO, B)
-    lifted = pltpu.VMEM((across[top][0], 2 * levels[top][1] * B + 2 * HALO, B), F32)
+    blocks, h = levels[top][1], levels[top][2]
+    long = 2 * blocks * B + 2 * HALO
+    bands = [(l[1] + 1, l[2] + 2 * HALO, B) for l in levels[1:]]
     between = pl.pallas_call(
         functools.partial(exchange_kernel, levels),
-        out_shape=[pltpu.VMEM(s, F32) for s in strips + across + [stack, across[0], stack]],
+        out_shape=[pltpu.VMEM(s, F32) for s in (
+            strips + [s[1:] for s in across] + [across[0][1:], (2 * blocks, 2 * h + 2 * HALO, B)])],
         in_specs=[hbm] * 5,
-        out_specs=[vmem] * 11,
+        out_specs=[vmem] * 10,
         scratch_shapes=[
             *[pltpu.VMEM((a, max(B, h), b * B), F32) for a, b, h in levels],
             *[pltpu.VMEM((2,) + s, F32) for s in across],
+            *[pltpu.VMEM(s, F32) for s in across],
+            *[pltpu.VMEM(s, F32) for s in strips],
+            *[pltpu.VMEM(s, F32) for s in bands],
+            *[pltpu.VMEM(s, F32) for s in across],
             pltpu.VMEM((4, B, B), F32),
             pltpu.VMEM((4, B, B), F32),
             pltpu.VMEM(stack, F32),
             pltpu.VMEM(stack, F32),
             pltpu.VMEM((2 * B + 2 * HALO, B), F32),
-            lifted,
+            pltpu.VMEM((across[top][0], long, B), F32),
             pltpu.VMEM((B, B), F32),
+            pltpu.VMEM((1 + sum(l[1] for l in levels), B, B), F32),
             pltpu.VMEM((2, row_count, B), F32),
             pltpu.VMEM((2, col_count, B), F32),
             pltpu.VMEM((4, 8, B), F32),
@@ -404,28 +512,24 @@
             pltpu.SemaphoreType.DMA((8,)),
         ],
         compiler_params=pltpu.CompilerParams(
-            collective_id=0, has_side_effects=True, vmem_limit_bytes=26 * 2**20),
+            collective_id=0, has_side_effects=True, vmem_limit_bytes=40 * 2**20),
     )(*[pltpu.with_memory_space_constraint(x, pltpu.HBM) for x in (coarse, d4, d3, d2, d1)])
-    blocks, h = levels[top][1], levels[top][2]
     return pl.pallas_call(
-        functools.partial(synthesis_kernel, levels),
+        functools.partial(strip_kernel, levels),
         out_shape=jax.ShapeDtypeStruct((2 * h, 2 * blocks * B), F32),
-        in_specs=[vmem] * 11,
+        in_specs=[vmem] * 10,
         out_specs=pl.BlockSpec(memory_space=pl.ANY),
         scratch_shapes=[
-            *[pltpu.VMEM((levels[k][1] + 1, levels[k][2] + 2 * HALO, B), F32) for k in (1, 2, 3)],
-            pltpu.VMEM((2 * blocks, 2 * h + 2 * HALO, B), F32),
-            *[pltpu.VMEM(s, F32) for s in strips],
-            *[pltpu.VMEM(s, F32) for s in across[1:]],
+            *[pltpu.VMEM((l[1] + 1, B, B), F32) for l in levels[1:]],
+            pltpu.VMEM((2, 2 * blocks, 16 * (strip_rows(top) // 8), B), F32),
+            pltpu.VMEM((2 * blocks, B, B), F32),
+            pltpu.VMEM((long, B), F32),
             pltpu.VMEM((B, B), F32),
-            pltpu.VMEM((B, B), F32),
-            pltpu.VMEM(stack, F32),
-            pltpu.VMEM((2 * B + 2 * HALO, B), F32),
-            lifted,
-            pltpu.VMEM((B, B), F32),
+            pltpu.VMEM(across[top][1:], F32),
             pltpu.SemaphoreType.DMA((2 * blocks,)),
+            pltpu.SemaphoreType.DMA((2, 2 * blocks)),
         ],
-        compiler_params=pltpu.CompilerParams(vmem_limit_bytes=28 * 2**20),
+        compiler_params=pltpu.CompilerParams(vmem_limit_bytes=12 * 2**20),
     )(*between)
 
 

time: 21.9 us -> 24.2 us (1.11)
  Pallas kernels: 21.8 us -> 24 us
    pallas_call x1, Pallas kernels: 13.8 us -> 20.4 us  [per_device(): pl.pallas_call(functools.partial(exchange_kernel, levels), out_shape=[plt...]
    pallas_call x1, Pallas kernels: 7.95 us -> 3.68 us  [per_device(): pl.pallas_call(functools.partial(strip_kernel, levels), out_shape=jax.Sha...]
where the time goes in v1:
time: 24.2 us; the launch traced here: 24.1 us
  Pallas kernels  24 us (99%)
    pallas_call x1, Pallas kernels, per_device(): pl.pallas_call(functools.partial(exchange_kernel, levels), out_shape=[plt...  20.4 us
    pallas_call x1, Pallas kernels, per_device(): pl.pallas_call(functools.partial(strip_kernel, levels), out_shape=jax.Sha...  3.68 us

profile of v1, /device:TPU:0, one launch (start us, length us, event | category | flops | bytes accessed | tf_op | source)
XLA Modules:
  0.0 24.1 jit_solution(16492374193881982601)
XLA Ops:
  0.0 20.4 %shard_map.55 = (f32[3,80,128]{2,1,0:T(8,128)S(1)}, f32[5,144,128]{2,1,0:T(8,128)S(1)}, f32[9,272,128]{2,1,0:T(8,128)S(1)}, f32[16,528,128]{2,1,0:T(8,128)S(1)},...) custom-call(f32[64,128]{1,0:T(8,128)} %refs_0_.1, ...), custom_call_target="tpu_custom_call" | custom-call | tf_op jit(solution)/shard_map/pallas_call | solution.py:483
  20.4 3.7 %shard_map.56 = f32[1024,2048]{1,0:T(8,128)} custom-call(f32[3,80,128]{2,1,0:T(8,128)S(1)} %get-tuple-element.15.refs_0_, f32[5,144,128]{2,1,0:T(8,128)S(1)} %get-tuple-element.16.refs_1_, f32[9,272,128]{2,1,0:T(8,128)S(1)} %get-tuple-element.17.refs_2_, f32[16,528,128]{2,1,0:T(8,128)S(1)} %get-tuple-element.18.refs_3_, ...), custom_call_target="tpu_custom_call" | custom-call | tf_op jit(solution)/shard_map/pallas_call | solution.py:517

commit v2 on v0

--- a/solution.py
+++ b/solution.py
@@ -176,15 +176,20 @@
     h = levels[0][2]
     load(coarse, ns[0].at[3, pl.ds(0, h), :])
     load(d4, ns[0].at[pl.ds(0, 3), pl.ds(0, h), :])
-    load(d3, ns[1])
-    load(d2, ns[2])
+    for k, src in ((1, d3), (2, d2), (3, d1)):
+        h = levels[k][2]
+        for at in (pl.ds(0, 8), pl.ds(h - 8, 8)):
+            load(src.at[:, at, :], ns[k].at[:, at, :])
+    edge_loads = len(loads)
+    for k, src in ((1, d3), (2, d2)):
+        inner = pl.ds(8, levels[k][2] - 16)
+        load(src.at[:, inner, :], ns[k].at[:, inner, :])
     _, blocks, h = levels[top]
     w = blocks * B
-    for at in (pl.ds(0, 8), pl.ds(h - 8, 8)):
-        load(d1.at[:, at, :], ns[top].at[:, at, :])
     inner = pl.ds(8, h - 16)
     for at in (pl.ds(0, B), pl.ds(w - B, B)):
         load(d1.at[:, inner, at], ns[top].at[:, inner, at])
+    side_loads = len(loads)
     for a in range(3):
         at = pl.ds(B, w - 2 * B)
         load(d1.at[a, inner, at], ns[top].at[a, inner, at])
@@ -197,20 +202,8 @@
         columns_of(k, a)[n, pl.ds(HALO + b * B, B), :] = scaled(
             ns[k][a, pl.ds(n * B, B), pl.ds(b * B, B)].T, scale)
 
-    for copy in loads[:4]:
+    for copy in loads[:edge_loads]:
         copy.wait()
-    for k in range(top):
-        for a in range(levels[k][0]):
-            for n in range(row_blocks(levels[k])):
-                for b in range(levels[k][1]):
-                    transpose(k, a, n, b)
-    for copy in loads[4:8]:
-        copy.wait()
-    for a in range(3):
-        for n in range(row_blocks(levels[top])):
-            for b in (0, levels[top][1] - 1):
-                transpose(top, a, n, b)
-
     rows, _ = row_plan(levels)
     for k, a, b, at in rows:
         depth, h = depth_of(levels, k), levels[k][2]
@@ -231,13 +224,7 @@
                 packed = jnp.where(
                     group == 31 - q, turn(ns[k][a, at, pl.ds((blocks - 1) * B, B)], -4 * q), packed)
         corners_out[d] = packed
-    columns, _ = column_plan(levels)
-    for k, a, n, at in columns:
-        depth, w = depth_of(levels, k), levels[k][1] * B
-        cols_out[0, pl.ds(at, depth), :] = columns_of(k, a)[n, pl.ds(HALO, depth), :]
-        cols_out[1, pl.ds(at, depth), :] = columns_of(k, a)[n, pl.ds(HALO + w - depth, depth), :]
-
-    pl.semaphore_wait(barrier, len(DIRS))
+
     sends = []
     for d, step in enumerate(DIRS):
         if d < 2:
@@ -249,10 +236,39 @@
         sends.append(pltpu.make_async_remote_copy(
             src_ref=src, dst_ref=dst, send_sem=send_sem.at[d], recv_sem=recv_sem.at[d],
             device_id=neighbour(step), device_id_type=MESH))
-    for d in (4, 5, 6, 7, 0, 1, 2, 3):
-        sends[d].start()
-
-    for copy in loads[8:]:
+
+    def enter():
+        pl.semaphore_wait(barrier, len(DIRS))
+        for d in (4, 5, 6, 7, 0, 1):
+            sends[d].start()
+
+    early = jnp.logical_or(r < 1, c < 2)
+    pl.when(jnp.logical_not(early))(enter)
+
+    for copy in loads[edge_loads : edge_loads + 2]:
+        copy.wait()
+    for k in range(top):
+        for a in range(levels[k][0]):
+            for n in range(row_blocks(levels[k])):
+                for b in range(levels[k][1]):
+                    transpose(k, a, n, b)
+    for copy in loads[edge_loads + 2 : side_loads]:
+        copy.wait()
+    for a in range(3):
+        for n in range(row_blocks(levels[top])):
+            for b in (0, levels[top][1] - 1):
+                transpose(top, a, n, b)
+    columns, _ = column_plan(levels)
+    for k, a, n, at in columns:
+        depth, w = depth_of(levels, k), levels[k][1] * B
+        cols_out[0, pl.ds(at, depth), :] = columns_of(k, a)[n, pl.ds(HALO, depth), :]
+        cols_out[1, pl.ds(at, depth), :] = columns_of(k, a)[n, pl.ds(HALO + w - depth, depth), :]
+
+    pl.when(early)(enter)
+    sends[2].start()
+    sends[3].start()
+
+    for copy in loads[side_loads:]:
         copy.wait()
 
     def middle(a, carry):
@@ -280,13 +296,15 @@
             lift_rows(levels[k][1] * B, xs[k].at[0, n], xs[k].at[1, n], part)
             turn_back(levels[k], k == top, n, part, edge, ws[k])
 
-    for d in (0, 1, 4, 5, 6, 7):
+    for d in (0, 1):
         sends[d].wait()
     offsets = stack_offsets(levels)
     for k, a, b, at in rows:
         depth, base = depth_of(levels, k), offsets[k] + 8 * b
         hn[a, pl.ds(base, depth), :] = rows_in[0, pl.ds(at, depth), :]
         hn[a, pl.ds(base + 8 - depth, depth), :] = rows_in[1, pl.ds(at, depth), :]
+    for d in (4, 5, 6, 7):
+        sends[d].wait()
     low, bottom = iota(1) < 64, iota(0) < 4
     for q, (k, a) in enumerate(arrays):
         tile = jnp.where(
@@ -310,7 +328,7 @@
     lows = (None,) + refs[12:15]
     image = refs[15]
     us, ts = refs[16:20], (c4,) + refs[20:23]
-    hn, cn, th, hd, lifted, edge, out_sem = refs[23:]
+    hn, cn, th, hd, lifted, edge, even, odd, out_sem = refs[23:]
     top = len(levels) - 1
     offsets = stack_offsets(levels)
     bottom = iota(0) < 4
@@ -345,22 +363,46 @@
         for n in range(n_rows):
             part = lifted.at[n, pl.ds(0, 2 * w + 16), :]
             lift_rows(w, ts[k].at[n], zs[k].at[n], part)
-            turn_back(level, final, n, part, edge, us[k])
+            if not final:
+                turn_back(level, final, n, part, edge, us[k])
         if not final:
             for j in range(2 * blocks + 1):
                 lift_rows(h, us[k].at[j], ws[k].at[j], lows[k + 1].at[j])
         else:
-            def body(j, carry, h=h):
-                lift_rows(h, us[top].at[j], ws[top].at[j], image.at[j])
+            def fill(j, dst):
+                dst[pl.ds(0, 8), :] = us[top][j, pl.ds(0, 8), :]
+                dst[pl.ds(HALO + h, 8), :] = us[top][j, pl.ds(HALO + h, 8), :]
+                at = pl.ds(pl.multiple_of(HALO + j * B, 8), B)
+                for n in range(n_rows):
+                    dst[pl.ds(HALO + n * B, B), :] = lifted[n, at, :].T
+
+            def finish(j, src, dst):
+                lift_rows(h, src, ws[top].at[j], dst)
+
+            def send(j, slot, src):
                 pltpu.make_async_copy(
-                    image.at[j, pl.ds(HALO, 2 * h), :],
-                    out.at[:, pl.ds(pl.multiple_of(j * B, B), B)], out_sem.at[j]).start()
+                    src.at[j, pl.ds(HALO, 2 * h), :],
+                    out.at[:, pl.ds(pl.multiple_of((2 * j + slot) * B, B), B)], out_sem.at[slot, j]).start()
+
+            last = 2 * blocks - 1
+            fill(0, even)
+
+            def body(i, carry):
+                j = 2 * i
+                fill(j + 1, odd)
+                finish(j, even, image.at[0, i])
+                send(i, 0, image.at[0])
+                fill(jnp.minimum(j + 2, last), even)
+                finish(j + 1, odd, image.at[1, i])
+                send(i, 1, image.at[1])
                 return carry
 
-            lax.fori_loop(0, 2 * blocks, body, 0)
-            for j in range(2 * blocks):
-                pltpu.make_async_copy(
-                    image.at[j, pl.ds(HALO, 2 * h), :], out.at[:, pl.ds(j * B, B)], out_sem.at[j]).wait()
+            lax.fori_loop(0, blocks, body, 0)
+            for i in range(blocks):
+                for slot in range(2):
+                    pltpu.make_async_copy(
+                        image.at[slot, i, pl.ds(HALO, 2 * h), :],
+                        out.at[:, pl.ds((2 * i + slot) * B, B)], out_sem.at[slot, i]).wait()
 
 
 def per_device(coarse, d4, d3, d2, d1):
@@ -399,7 +441,7 @@
             pltpu.VMEM((2, row_count, B), F32),
             pltpu.VMEM((2, col_count, B), F32),
             pltpu.VMEM((4, 8, B), F32),
-            pltpu.SemaphoreType.DMA((11,)),
+            pltpu.SemaphoreType.DMA((15,)),
             pltpu.SemaphoreType.DMA((8,)),
             pltpu.SemaphoreType.DMA((8,)),
         ],
@@ -414,7 +456,7 @@
         out_specs=pl.BlockSpec(memory_space=pl.ANY),
         scratch_shapes=[
             *[pltpu.VMEM((levels[k][1] + 1, levels[k][2] + 2 * HALO, B), F32) for k in (1, 2, 3)],
-            pltpu.VMEM((2 * blocks, 2 * h + 2 * HALO, B), F32),
+            pltpu.VMEM((2, blocks, 2 * h + 2 * HALO, B), F32),
             *[pltpu.VMEM(s, F32) for s in strips],
             *[pltpu.VMEM(s, F32) for s in across[1:]],
             pltpu.VMEM((B, B), F32),
@@ -423,7 +465,9 @@
             pltpu.VMEM((2 * B + 2 * HALO, B), F32),
             lifted,
             pltpu.VMEM((B, B), F32),
-            pltpu.SemaphoreType.DMA((2 * blocks,)),
+            pltpu.VMEM(strips[top][1:], F32),
+            pltpu.VMEM(strips[top][1:], F32),
+            pltpu.SemaphoreType.DMA((2, blocks)),
         ],
         compiler_params=pltpu.CompilerParams(vmem_limit_bytes=28 * 2**20),
     )(*between)

time: 21.9 us -> 21.2 us (0.968)
  Pallas kernels: 21.8 us -> 21.1 us
    pallas_call x1, Pallas kernels: 7.95 us -> 7.16 us  [per_device(): pl.pallas_call(functools.partial(synthesis_kernel, levels), out_shape=jax...]
where the time goes in v2:
time: 21.2 us; the launch traced here: 21.1 us
  Pallas kernels  21.1 us (100%)
    pallas_call x1, Pallas kernels, per_device(): pl.pallas_call(functools.partial(exchange_kernel, levels), out_shape=[plt...  13.9 us
    pallas_call x1, Pallas kernels, per_device(): pl.pallas_call(functools.partial(synthesis_kernel, levels), out_shape=jax...  7.16 us

profile of v2, /device:TPU:0, one launch (start us, length us, event | category | flops | bytes accessed | tf_op | source)
XLA Modules:
  0.0 21.1 jit_solution(10092175500322772462)
XLA Ops:
  0.0 13.9 %shard_map.55 = (f32[3,80,128]{2,1,0:T(8,128)S(1)}, f32[5,144,128]{2,1,0:T(8,128)S(1)}, f32[9,272,128]{2,1,0:T(8,128)S(1)}, f32[16,528,128]{2,1,0:T(8,128)S(1)},...) custom-call(f32[64,128]{1,0:T(8,128)} %refs_0_.1, ...), custom_call_target="tpu_custom_call" | custom-call | tf_op jit(solution)/shard_map/pallas_call | solution.py:423
  13.9 7.2 %shard_map.56 = f32[1024,2048]{1,0:T(8,128)} custom-call(f32[3,80,128]{2,1,0:T(8,128)S(1)} %get-tuple-element.16.refs_0_, f32[5,144,128]{2,1,0:T(8,128)S(1)} %get-tuple-element.17.refs_1_, f32[9,272,128]{2,1,0:T(8,128)S(1)} %get-tuple-element.18.refs_2_, f32[16,528,128]{2,1,0:T(8,128)S(1)} %get-tuple-element.19.refs_3_, ...), custom_call_target="tpu_custom_call" | custom-call | tf_op jit(solution)/shard_map/pallas_call | solution.py:452

commit v3 on v2

--- a/solution.py
+++ b/solution.py
@@ -69,10 +69,13 @@
 
 
 def lift_rows(count, s, r, dst):
-    run = (count + 8) // 8
-
+    lift_runs((count + 8) // 8, s, HALO - 4, r, HALO - 4, dst)
+
+
+def lift_runs(run, s, s_at, r, r_at, dst):
     def rows(ref, t):
-        return ref[pl.ds(HALO - 4 + t, 8, stride=run), :]
+        at = s_at if ref is s else r_at
+        return ref[pl.ds(at + t, 8, stride=run), :]
 
     r0, s1, r1, s2 = {}, {}, {}, {}
     for t in range(-2, run + 2):
@@ -97,16 +100,19 @@
     return x if scale is None else x * scale
 
 
-def turn_back(level, final, n, lifted, edge, dst):
+def turn_back(level, n, lifted, dst, which):
+    count = min(B, level[2])
+    at = pl.ds(HALO + n * B, count)
+    for j in which:
+        dst[j, at, :] = lifted[pl.ds(HALO + j * B, B), :].T[:count]
+
+
+def turn_back_side(level, n, lifted, edge, dst):
     _, blocks, h = level
     count = min(B, h)
-    at = pl.ds(HALO + n * B, count)
-    for j in range(2 * blocks):
-        dst[j, at, :] = lifted[pl.ds(HALO + j * B, B), :].T[:count]
-    if not final:
-        edge[0:8, :] = lifted[pl.ds(HALO + 2 * blocks * B, 8), :]
-        edge[B - 8 : B, :] = lifted[0:8, :]
-        dst[2 * blocks, at, :] = edge[...].T[:count]
+    edge[0:8, :] = lifted[pl.ds(HALO + 2 * blocks * B, 8), :]
+    edge[B - 8 : B, :] = lifted[0:8, :]
+    dst[2 * blocks, pl.ds(HALO + n * B, count), :] = edge[...].T[:count]
 
 
 def halo_transpose(levels, hn, cn, scale, dst):
@@ -153,8 +159,9 @@
     ws, zs = refs[5:9], refs[9:13]
     zh, c4, ch = refs[13:16]
     ns, xs = refs[16:20], refs[20:24]
-    (hn, cn, sh, rh, hd, lifted, edge, rows_out, cols_out, corners_out, rows_in, cols_in, corners_in,
-     load_sem, send_sem, recv_sem) = refs[24:]
+    ls = refs[24:28]
+    (hn, cn, sh, rh, hd, edge, rows_out, cols_out, corners_out, rows_in, cols_in, corners_in,
+     load_sem, send_sem, recv_sem) = refs[28:]
     nr, nc = lax.axis_size("rows"), lax.axis_size("cols")
     r, c = lax.axis_index("rows"), lax.axis_index("cols")
     top = len(levels) - 1
@@ -242,47 +249,64 @@
         for d in (4, 5, 6, 7, 0, 1):
             sends[d].start()
 
-    early = jnp.logical_or(r < 1, c < 2)
+    early = jnp.logical_or(r < 1, c < 1)
     pl.when(jnp.logical_not(early))(enter)
 
-    for copy in loads[edge_loads : edge_loads + 2]:
+    for copy in loads[edge_loads:side_loads]:
         copy.wait()
-    for k in range(top):
+
+    def blocks_of(k, which):
+        blocks = levels[k][1]
+        sides = sorted({0, blocks - 1})
+        return sides if which == "sides" else range(1, blocks - 1)
+
+    for k in range(top + 1):
         for a in range(levels[k][0]):
             for n in range(row_blocks(levels[k])):
-                for b in range(levels[k][1]):
+                for b in blocks_of(k, "sides"):
                     transpose(k, a, n, b)
-    for copy in loads[edge_loads + 2 : side_loads]:
-        copy.wait()
-    for a in range(3):
-        for n in range(row_blocks(levels[top])):
-            for b in (0, levels[top][1] - 1):
-                transpose(top, a, n, b)
     columns, _ = column_plan(levels)
     for k, a, n, at in columns:
         depth, w = depth_of(levels, k), levels[k][1] * B
         cols_out[0, pl.ds(at, depth), :] = columns_of(k, a)[n, pl.ds(HALO, depth), :]
         cols_out[1, pl.ds(at, depth), :] = columns_of(k, a)[n, pl.ds(HALO + w - depth, depth), :]
 
-    pl.when(early)(enter)
-    sends[2].start()
-    sends[3].start()
-
+    def enter_sides():
+        sends[2].start()
+        sends[3].start()
+
+    pl.when(jnp.logical_not(early))(enter_sides)
+
+    for k in range(top):
+        for a in range(levels[k][0]):
+            for n in range(row_blocks(levels[k])):
+                for b in blocks_of(k, "middle"):
+                    transpose(k, a, n, b)
     for copy in loads[side_loads:]:
         copy.wait()
 
     def middle(a, carry):
         for n in range(row_blocks(levels[top])):
-            for b in range(1, levels[top][1] - 1):
+            for b in blocks_of(top, "middle"):
                 at = pl.ds(HALO + b * B, B)
                 block = ns[top][a, pl.ds(n * B, B), pl.ds(b * B, B)].T
                 xs[top][a - 1, n, at, :] = block * jnp.where(a == 2, F32(DOWN2), F32(1.0))
         return carry
 
     for n in range(row_blocks(levels[top])):
-        for b in range(1, levels[top][1] - 1):
+        for b in blocks_of(top, "middle"):
             transpose(top, 0, n, b)
     lax.fori_loop(1, 3, middle, 0)
+    for k in (3, 2, 1, 0):
+        for n in range(row_blocks(levels[k])):
+            lift_rows(levels[k][1] * B, xs[k].at[0, n], xs[k].at[1, n], ls[k].at[n])
+            turn_back(levels[k], n, ls[k].at[n], ws[k], range(1, 2 * levels[k][1] - 1))
+
+    def enter_late():
+        enter()
+        enter_sides()
+
+    pl.when(early)(enter_late)
 
     sends[2].wait()
     sends[3].wait()
@@ -291,10 +315,15 @@
         columns_of(k, a)[n, pl.ds(HALO + w, depth), :] = cols_in[0, pl.ds(at, depth), :]
         columns_of(k, a)[n, pl.ds(HALO - depth, depth), :] = cols_in[1, pl.ds(at, depth), :]
     for k in (3, 2, 1, 0):
+        blocks = levels[k][1]
+        w = blocks * B
         for n in range(row_blocks(levels[k])):
-            part = lifted.at[n, pl.ds(0, 2 * levels[k][1] * B + 16), :]
-            lift_rows(levels[k][1] * B, xs[k].at[0, n], xs[k].at[1, n], part)
-            turn_back(levels[k], k == top, n, part, edge, ws[k])
+            part = ls[k].at[n]
+            for at in (HALO - 4, HALO + w - 4):
+                lift_runs(1, xs[k].at[0, n], at, xs[k].at[1, n], at, ls[k].at[n, pl.ds(2 * at - HALO, 16), :])
+            turn_back(levels[k], n, part, ws[k], (0, 2 * blocks - 1))
+            if k < top:
+                turn_back_side(levels[k], n, part, edge, ws[k])
 
     for d in (0, 1):
         sends[d].wait()
@@ -328,7 +357,7 @@
     lows = (None,) + refs[12:15]
     image = refs[15]
     us, ts = refs[16:20], (c4,) + refs[20:23]
-    hn, cn, th, hd, lifted, edge, even, odd, out_sem = refs[23:]
+    hn, cn, th, hd, lifted, edge, out_sem = refs[23:]
     top = len(levels) - 1
     offsets = stack_offsets(levels)
     bottom = iota(0) < 4
@@ -338,6 +367,14 @@
         w = blocks * B
         final = k == top
         n_rows = row_blocks(level)
+        def columns_from(n):
+            at = pl.ds(HALO + n * B, B)
+            for b in range(blocks):
+                ts[k][n, pl.ds(HALO + b * B, B), :] = low[b, at, :].T * UP2
+            side = low[blocks, at, :].T * UP2
+            ts[k][n, pl.ds(0, 8), :] = side[B - 8 :]
+            ts[k][n, pl.ds(HALO + w, 8), :] = side[:8]
+
         if k == 0:
             halo = ch
         else:
@@ -351,58 +388,57 @@
                     cn[pl.ds(offsets[k], 8), :] = tile
                     cn[pl.ds(offsets[k] + 8 * (blocks - 1), 8), :] = tile
             halo_transpose(levels, hn, cn, UP2, th)
-            for n in range(n_rows):
-                at = pl.ds(HALO + n * B, B)
-                for b in range(blocks):
-                    ts[k][n, pl.ds(HALO + b * B, B), :] = low[b, at, :].T * UP2
-                side = low[blocks, at, :].T * UP2
-                ts[k][n, pl.ds(0, 8), :] = side[B - 8 :]
-                ts[k][n, pl.ds(HALO + w, 8), :] = side[:8]
         lift_rows(B, halo, zh, hd)
         halo_back(levels, (k,), hd, edge, {k: us[k]})
-        for n in range(n_rows):
-            part = lifted.at[n, pl.ds(0, 2 * w + 16), :]
-            lift_rows(w, ts[k].at[n], zs[k].at[n], part)
-            if not final:
-                turn_back(level, final, n, part, edge, us[k])
         if not final:
+            for n in range(n_rows):
+                if k > 0:
+                    columns_from(n)
+                part = lifted.at[n, pl.ds(0, 2 * w + 16), :]
+                lift_rows(w, ts[k].at[n], zs[k].at[n], part)
+                turn_back(level, n, part, us[k], range(2 * blocks))
+                turn_back_side(level, n, part, edge, us[k])
             for j in range(2 * blocks + 1):
                 lift_rows(h, us[k].at[j], ws[k].at[j], lows[k + 1].at[j])
-        else:
-            def fill(j, dst):
-                dst[pl.ds(0, 8), :] = us[top][j, pl.ds(0, 8), :]
-                dst[pl.ds(HALO + h, 8), :] = us[top][j, pl.ds(HALO + h, 8), :]
-                at = pl.ds(pl.multiple_of(HALO + j * B, 8), B)
-                for n in range(n_rows):
-                    dst[pl.ds(HALO + n * B, B), :] = lifted[n, at, :].T
-
-            def finish(j, src, dst):
-                lift_rows(h, src, ws[top].at[j], dst)
-
-            def send(j, slot, src):
-                pltpu.make_async_copy(
-                    src.at[j, pl.ds(HALO, 2 * h), :],
-                    out.at[:, pl.ds(pl.multiple_of((2 * j + slot) * B, B), B)], out_sem.at[slot, j]).start()
-
-            last = 2 * blocks - 1
-            fill(0, even)
-
-            def body(i, carry):
-                j = 2 * i
-                fill(j + 1, odd)
-                finish(j, even, image.at[0, i])
-                send(i, 0, image.at[0])
-                fill(jnp.minimum(j + 2, last), even)
-                finish(j + 1, odd, image.at[1, i])
-                send(i, 1, image.at[1])
-                return carry
-
-            lax.fori_loop(0, blocks, body, 0)
-            for i in range(blocks):
-                for slot in range(2):
-                    pltpu.make_async_copy(
-                        image.at[slot, i, pl.ds(HALO, 2 * h), :],
-                        out.at[:, pl.ds((2 * i + slot) * B, B)], out_sem.at[slot, i]).wait()
+            continue
+
+        half = n_rows // 2
+        run = half * B // 8 - 1
+        seam = 8 * run - 4
+        runs = (run, (h + 4 - seam) // 8)
+        ats = (HALO - 4, HALO + seam)
+        dsts = (pl.ds(0, 16 * run), pl.ds(16 * run, 16 * runs[1]))
+        outs = (pl.ds(0, 2 * seam), pl.ds(2 * seam, 2 * (h - seam)))
+
+        def image_copy(part, j):
+            row = (HALO, HALO + 2 * seam)[part]
+            return pltpu.make_async_copy(
+                image.at[j, pl.ds(row, outs[part].size), :],
+                out.at[outs[part], pl.ds(j * B, B)], out_sem.at[part, j])
+
+        last = 2 * blocks - 1
+
+        for part in range(2):
+            these = (range(half), range(half, n_rows))[part]
+            for n in these:
+                columns_from(n)
+                lift_rows(w, ts[k].at[n], zs[k].at[n], lifted.at[n])
+
+            def fill(j, these=these):
+                for n in these:
+                    us[top][j, pl.ds(HALO + n * B, B), :] = lifted[n, pl.ds(HALO + j * B, B), :].T
+
+            fill(0)
+            for j in range(2 * blocks):
+                if j < last:
+                    fill(j + 1)
+                lift_runs(runs[part], us[top].at[j], ats[part], ws[top].at[j], ats[part],
+                          image.at[j, dsts[part], :])
+                image_copy(part, j).start()
+
+        for part in range(2):
+            for j in range(2 * blocks):
+                image_copy(part, j).wait()
 
 
 def per_device(coarse, d4, d3, d2, d1):
@@ -428,12 +464,12 @@
         scratch_shapes=[
             *[pltpu.VMEM((a, max(B, h), b * B), F32) for a, b, h in levels],
             *[pltpu.VMEM((2,) + s, F32) for s in across],
+            *[pltpu.VMEM((n, 2 * l[1] * B + 2 * HALO, B), F32) for (n, _, _), l in zip(across, levels)],
             pltpu.VMEM((4, B, B), F32),
             pltpu.VMEM((4, B, B), F32),
             pltpu.VMEM(stack, F32),
             pltpu.VMEM(stack, F32),
             pltpu.VMEM((2 * B + 2 * HALO, B), F32),
-            lifted,
             pltpu.VMEM((B, B), F32),
             pltpu.VMEM((2, row_count, B), F32),
             pltpu.VMEM((2, col_count, B), F32),
@@ -446,7 +482,7 @@
             pltpu.SemaphoreType.DMA((8,)),
         ],
         compiler_params=pltpu.CompilerParams(
-            collective_id=0, has_side_effects=True, vmem_limit_bytes=26 * 2**20),
+            collective_id=0, has_side_effects=True, vmem_limit_bytes=30 * 2**20),
     )(*[pltpu.with_memory_space_constraint(x, pltpu.HBM) for x in (coarse, d4, d3, d2, d1)])
     blocks, h = levels[top][1], levels[top][2]
     return pl.pallas_call(
@@ -456,7 +492,7 @@
         out_specs=pl.BlockSpec(memory_space=pl.ANY),
         scratch_shapes=[
             *[pltpu.VMEM((levels[k][1] + 1, levels[k][2] + 2 * HALO, B), F32) for k in (1, 2, 3)],
-            pltpu.VMEM((2, blocks, 2 * h + 2 * HALO, B), F32),
+            pltpu.VMEM((2 * blocks, 2 * h + 2 * HALO, B), F32),
             *[pltpu.VMEM(s, F32) for s in strips],
             *[pltpu.VMEM(s, F32) for s in across[1:]],
             pltpu.VMEM((B, B), F32),
@@ -465,9 +501,7 @@
             pltpu.VMEM((2 * B + 2 * HALO, B), F32),
             lifted,
             pltpu.VMEM((B, B), F32),
-            pltpu.VMEM(strips[top][1:], F32),
-            pltpu.VMEM(strips[top][1:], F32),
-            pltpu.SemaphoreType.DMA((2, blocks)),
+            pltpu.SemaphoreType.DMA((2, 2 * blocks)),
         ],
         compiler_params=pltpu.CompilerParams(vmem_limit_bytes=28 * 2**20),
     )(*between)

time: 21.2 us -> 22.7 us (1.071)
  Pallas kernels: 21.1 us -> 22.6 us
    pallas_call x1, Pallas kernels: 13.9 us -> 15.4 us  [per_device(): pl.pallas_call(functools.partial(exchange_kernel, levels), out_shape=[plt...]
where the time goes in v3:
time: 22.7 us; the launch traced here: 22.6 us
  Pallas kernels  22.6 us (100%)
    pallas_call x1, Pallas kernels, per_device(): pl.pallas_call(functools.partial(exchange_kernel, levels), out_shape=[plt...  15.4 us
    pallas_call x1, Pallas kernels, per_device(): pl.pallas_call(functools.partial(synthesis_kernel, levels), out_shape=jax...  7.19 us

profile of v3, /device:TPU:0, one launch (start us, length us, event | category | flops | bytes accessed | tf_op | source)
XLA Modules:
  0.0 22.6 jit_solution(18056163787841351525)
XLA Ops:
  0.0 15.4 %shard_map.55 = (f32[3,80,128]{2,1,0:T(8,128)S(1)}, f32[5,144,128]{2,1,0:T(8,128)S(1)}, f32[9,272,128]{2,1,0:T(8,128)S(1)}, f32[16,528,128]{2,1,0:T(8,128)S(1)},...) custom-call(f32[64,128]{1,0:T(8,128)} %refs_0_.1, ...), custom_call_target="tpu_custom_call" | custom-call | tf_op jit(solution)/shard_map/pallas_call | solution.py:459
  15.4 7.2 %shard_map.56 = f32[1024,2048]{1,0:T(8,128)} custom-call(f32[3,80,128]{2,1,0:T(8,128)S(1)} %get-tuple-element.16.refs_0_, f32[5,144,128]{2,1,0:T(8,128)S(1)} %get-tuple-element.17.refs_1_, f32[9,272,128]{2,1,0:T(8,128)S(1)} %get-tuple-element.18.refs_2_, f32[16,528,128]{2,1,0:T(8,128)S(1)} %get-tuple-element.19.refs_3_, ...), custom_call_target="tpu_custom_call" | custom-call | tf_op jit(solution)/shard_map/pallas_call | solution.py:488

commit v4 on v1

--- a/solution.py
+++ b/solution.py
@@ -100,16 +100,19 @@
     return x if scale is None else x * scale
 
 
-def turn_back(level, final, n, lifted, edge, dst):
+def turn_back(level, n, lifted, dst, which):
+    count = min(B, level[2])
+    at = pl.ds(HALO + n * B, count)
+    for j in which:
+        dst[j, at, :] = lifted[pl.ds(HALO + j * B, B), :].T[:count]
+
+
+def turn_back_side(level, n, lifted, edge, dst):
     _, blocks, h = level
     count = min(B, h)
-    at = pl.ds(HALO + n * B, count)
-    for j in range(2 * blocks):
-        dst[j, at, :] = lifted[pl.ds(HALO + j * B, B), :].T[:count]
-    if not final:
-        edge[0:8, :] = lifted[pl.ds(HALO + 2 * blocks * B, 8), :]
-        edge[B - 8 : B, :] = lifted[0:8, :]
-        dst[2 * blocks, at, :] = edge[...].T[:count]
+    edge[0:8, :] = lifted[pl.ds(HALO + 2 * blocks * B, 8), :]
+    edge[B - 8 : B, :] = lifted[0:8, :]
+    dst[2 * blocks, pl.ds(HALO + n * B, count), :] = edge[...].T[:count]
 
 
 def halo_transpose(levels, hn, cn, scale, dst):
@@ -176,25 +179,21 @@
     return b if a == 3 else 1 + sum(l[1] for l in levels[:k]) + b
 
 
-def columns_from(level, low, dst):
-    _, blocks, _ = level
-    for n in range(row_blocks(level)):
-        at = pl.ds(HALO + n * B, B)
-        for b in range(blocks):
-            dst[n, pl.ds(HALO + b * B, B), :] = low[b, at, :].T * UP2
-        side = low[blocks, at, :].T * UP2
-        dst[n, pl.ds(0, 8), :] = side[B - 8 :]
-        dst[n, pl.ds(HALO + blocks * B, 8), :] = side[:8]
+def side_takes(levels, k):
+    if k == len(levels) - 1:
+        return 64, 8, 72
+    take = 8 + strip_rows(k + 1)
+    return take, 0, take
 
 
 def exchange_kernel(levels, *refs):
     coarse, d4, d3, d2, d1 = refs[:5]
     ws, zts, ct_out, image = refs[5:9], refs[9:13], refs[13], refs[14]
-    ns, xs, zs, us = refs[15:19], refs[19:23], refs[23:27], refs[27:31]
-    lows, ts = (None,) + refs[31:34], refs[34:38]
-    c4 = ts[0]
-    (hn, cn, sh, rh, hd, lifted, edge, ds, rows_out, cols_out, corners_out, rows_in, cols_in, corners_in,
-     load_sem, send_sem, recv_sem) = refs[38:]
+    zs, c4, wcs = refs[15:19], refs[19], refs[20:24]
+    ns, xs, ls, us = refs[24:28], refs[28:32], refs[32:36], refs[36:40]
+    lows, ts = (None,) + refs[40:43], (c4,) + refs[43:46]
+    (hn, cn, sh, rh, hd, lifted, edge, ds, even, odd, rows_out, cols_out, corners_out,
+     rows_in, cols_in, corners_in, load_sem, send_sem, recv_sem) = refs[46:]
     nr, nc = lax.axis_size("rows"), lax.axis_size("cols")
     r, c = lax.axis_index("rows"), lax.axis_index("cols")
     top = len(levels) - 1
@@ -216,15 +215,20 @@
     h = levels[0][2]
     load(coarse, ns[0].at[3, pl.ds(0, h), :])
     load(d4, ns[0].at[pl.ds(0, 3), pl.ds(0, h), :])
-    load(d3, ns[1])
-    load(d2, ns[2])
+    for k, src in ((1, d3), (2, d2), (3, d1)):
+        h = levels[k][2]
+        for at in (pl.ds(0, 8), pl.ds(h - 8, 8)):
+            load(src.at[:, at, :], ns[k].at[:, at, :])
+    edge_loads = len(loads)
+    for k, src in ((1, d3), (2, d2)):
+        inner = pl.ds(8, levels[k][2] - 16)
+        load(src.at[:, inner, :], ns[k].at[:, inner, :])
     _, blocks, h = levels[top]
     w = blocks * B
-    for at in (pl.ds(0, 8), pl.ds(h - 8, 8)):
-        load(d1.at[:, at, :], ns[top].at[:, at, :])
     inner = pl.ds(8, h - 16)
     for at in (pl.ds(0, B), pl.ds(w - B, B)):
         load(d1.at[:, inner, at], ns[top].at[:, inner, at])
+    side_loads = len(loads)
     for a in range(3):
         at = pl.ds(B, w - 2 * B)
         load(d1.at[a, inner, at], ns[top].at[a, inner, at])
@@ -237,20 +241,8 @@
         columns_of(k, a)[n, pl.ds(HALO + b * B, B), :] = scaled(
             ns[k][a, pl.ds(n * B, B), pl.ds(b * B, B)].T, scale)
 
-    for copy in loads[:4]:
+    for copy in loads[:edge_loads]:
         copy.wait()
-    for k in range(top):
-        for a in range(levels[k][0]):
-            for n in range(row_blocks(levels[k])):
-                for b in range(levels[k][1]):
-                    transpose(k, a, n, b)
-    for copy in loads[4:8]:
-        copy.wait()
-    for a in range(3):
-        for n in range(row_blocks(levels[top])):
-            for b in (0, levels[top][1] - 1):
-                transpose(top, a, n, b)
-
     rows, _ = row_plan(levels)
     for k, a, b, at in rows:
         depth, h = depth_of(levels, k), levels[k][2]
@@ -271,13 +263,7 @@
                 packed = jnp.where(
                     group == 31 - q, turn(ns[k][a, at, pl.ds((blocks - 1) * B, B)], -4 * q), packed)
         corners_out[d] = packed
-    columns, _ = column_plan(levels)
-    for k, a, n, at in columns:
-        depth, w = depth_of(levels, k), levels[k][1] * B
-        cols_out[0, pl.ds(at, depth), :] = columns_of(k, a)[n, pl.ds(HALO, depth), :]
-        cols_out[1, pl.ds(at, depth), :] = columns_of(k, a)[n, pl.ds(HALO + w - depth, depth), :]
-
-    pl.semaphore_wait(barrier, len(DIRS))
+
     sends = []
     for d, step in enumerate(DIRS):
         if d < 2:
@@ -289,24 +275,122 @@
         sends.append(pltpu.make_async_remote_copy(
             src_ref=src, dst_ref=dst, send_sem=send_sem.at[d], recv_sem=recv_sem.at[d],
             device_id=neighbour(step), device_id_type=MESH))
-    for d in (4, 5, 6, 7, 0, 1, 2, 3):
-        sends[d].start()
-
-    for copy in loads[8:]:
+
+    def enter():
+        pl.semaphore_wait(barrier, len(DIRS))
+        for d in (4, 5, 6, 7, 0, 1):
+            sends[d].start()
+
+    def enter_sides():
+        sends[2].start()
+        sends[3].start()
+
+    def enter_all():
+        enter()
+        enter_sides()
+
+    first_row = r < 1
+    fourth = jnp.logical_and(first_row, c < 2)
+    third = jnp.logical_or(
+        jnp.logical_and(first_row, c >= 2),
+        jnp.logical_and(jnp.logical_and(lax.rem(r, 4) < 1, r >= 1), c < 1))
+    rest = jnp.logical_not(jnp.logical_or(third, fourth))
+    quick = jnp.logical_or(jnp.logical_and(c >= 2, lax.rem(c, 2) < 1), c >= nc - 1)
+    at_once = jnp.logical_and(rest, quick)
+    second = jnp.logical_and(rest, jnp.logical_not(quick))
+    pl.when(at_once)(enter)
+
+    for copy in loads[edge_loads:side_loads]:
+        copy.wait()
+
+    def blocks_of(k, which):
+        blocks = levels[k][1]
+        sides = sorted({0, blocks - 1})
+        return sides if which == "sides" else range(1, blocks - 1)
+
+    for k in range(top + 1):
+        for a in range(levels[k][0]):
+            for n in range(row_blocks(levels[k])):
+                for b in blocks_of(k, "sides"):
+                    transpose(k, a, n, b)
+    columns, _ = column_plan(levels)
+    for k, a, n, at in columns:
+        depth, w = depth_of(levels, k), levels[k][1] * B
+        cols_out[0, pl.ds(at, depth), :] = columns_of(k, a)[n, pl.ds(HALO, depth), :]
+        cols_out[1, pl.ds(at, depth), :] = columns_of(k, a)[n, pl.ds(HALO + w - depth, depth), :]
+
+    pl.when(at_once)(enter_sides)
+    pl.when(second)(enter_all)
+
+    for k in range(top):
+        for a in range(levels[k][0]):
+            for n in range(row_blocks(levels[k])):
+                for b in blocks_of(k, "middle"):
+                    transpose(k, a, n, b)
+    for copy in loads[side_loads:]:
         copy.wait()
 
     def middle(a, carry):
         for n in range(row_blocks(levels[top])):
-            for b in range(1, levels[top][1] - 1):
+            for b in blocks_of(top, "middle"):
                 at = pl.ds(HALO + b * B, B)
                 block = ns[top][a, pl.ds(n * B, B), pl.ds(b * B, B)].T
                 xs[top][a - 1, n, at, :] = block * jnp.where(a == 2, F32(DOWN2), F32(1.0))
         return carry
 
     for n in range(row_blocks(levels[top])):
-        for b in range(1, levels[top][1] - 1):
+        for b in blocks_of(top, "middle"):
             transpose(top, 0, n, b)
     lax.fori_loop(1, 3, middle, 0)
+    for k in (3, 2, 1, 0):
+        for n in range(row_blocks(levels[k])):
+            lift_rows(levels[k][1] * B, xs[k].at[0, n], xs[k].at[1, n], ls[k].at[n])
+            turn_back(levels[k], n, ls[k].at[n], ws[k], range(2 * levels[k][1]))
+
+    pl.when(third)(enter_all)
+
+    for k, level in enumerate(levels):
+        _, blocks, h = level
+        w = blocks * B
+        n_rows = row_blocks(level)
+        for n in range(n_rows):
+            if k > 0:
+                for b in range(blocks):
+                    ts[k][n, pl.ds(HALO + b * B, B), :] = lows[k][b, pl.ds(HALO + n * B, B), :].T * UP2
+            part = lifted.at[n, pl.ds(0, 2 * w + 16), :]
+            lift_rows(w, ts[k].at[n], zs[k].at[n], part)
+            if k < top:
+                turn_back(level, n, part, us[k], range(2 * blocks))
+        if k < top:
+            for j in range(2 * blocks):
+                lift_rows(h, us[k].at[j], ws[k].at[j], lows[k + 1].at[j])
+        if k == top - 1:
+            pl.when(fourth)(enter_all)
+
+    def fill(j, dst):
+        at = pl.ds(pl.multiple_of(HALO + j * B, 8), B)
+        for n in range(row_blocks(levels[top])):
+            dst[pl.ds(HALO + n * B, B), :] = lifted[n, at, :].T
+
+    def body(i, carry):
+        j = 2 * i
+        _, blocks, h = levels[top]
+        fill(j + 1, odd)
+        lift_rows(h, even, ws[top].at[j], image.at[j])
+        fill(jnp.minimum(j + 2, 2 * blocks - 1), even)
+        lift_rows(h, odd, ws[top].at[j + 1], image.at[j + 1])
+        return carry
+
+    fill(0, even)
+    lax.fori_loop(0, levels[top][1], body, 0)
+
+    for k, (_, blocks, h) in enumerate(levels):
+        keep = strip_rows(k)
+        for a in (0, 3) if k == 0 else (0,):
+            for b in range(blocks):
+                at = pl.ds(b * B, B)
+                ds[at_of(levels, k, a, b), pl.ds(8, keep), :] = ns[k][a, pl.ds(0, keep), at]
+                ds[at_of(levels, k, a, b), pl.ds(8 + keep, keep), :] = ns[k][a, pl.ds(h - keep, keep), at]
 
     sends[2].wait()
     sends[3].wait()
@@ -315,45 +399,30 @@
         columns_of(k, a)[n, pl.ds(HALO + w, depth), :] = cols_in[0, pl.ds(at, depth), :]
         columns_of(k, a)[n, pl.ds(HALO - depth, depth), :] = cols_in[1, pl.ds(at, depth), :]
     for k in (3, 2, 1, 0):
+        blocks = levels[k][1]
+        w = blocks * B
         for n in range(row_blocks(levels[k])):
-            part = lifted.at[n, pl.ds(0, 2 * levels[k][1] * B + 16), :]
-            lift_rows(levels[k][1] * B, xs[k].at[0, n], xs[k].at[1, n], part)
-            turn_back(levels[k], k == top, n, part, edge, ws[k])
-
-    for k, level in enumerate(levels):
-        _, blocks, h = level
-        w = blocks * B
-        if k > 0:
-            columns_from(level, lows[k], ts[k])
-        for n in range(row_blocks(level)):
-            part = lifted.at[n, pl.ds(0, 2 * w + 16), :]
-            lift_rows(w, ts[k].at[n], zs[k].at[n], part)
-            turn_back(level, k == top, n, part, edge, us[k])
-        if k < top:
-            for j in range(2 * blocks + 1):
-                lift_rows(h, us[k].at[j], ws[k].at[j], lows[k + 1].at[j])
-        else:
-            def body(j, carry, h=h):
-                lift_rows(h, us[top].at[j], ws[top].at[j], image.at[j])
-                return carry
-
-            lax.fori_loop(0, 2 * blocks, body, 0)
-
-    for k, (_, blocks, h) in enumerate(levels):
-        keep = strip_rows(k)
-        for a in (0, 3) if k == 0 else (0,):
-            for b in range(blocks):
-                at = pl.ds(b * B, B)
-                ds[at_of(levels, k, a, b), pl.ds(8, keep), :] = ns[k][a, pl.ds(0, keep), at]
-                ds[at_of(levels, k, a, b), pl.ds(8 + keep, keep), :] = ns[k][a, pl.ds(h - keep, keep), at]
-
-    for d in (0, 1, 4, 5, 6, 7):
+            part = ls[k].at[n]
+            for at in (HALO - 4, HALO + w - 4):
+                lift_runs(1, xs[k].at[0, n], at, xs[k].at[1, n], at, ls[k].at[n, pl.ds(2 * at - HALO, 16), :])
+            turn_back(levels[k], n, part, ws[k], (0, 2 * blocks - 1))
+            if k < top:
+                turn_back_side(levels[k], n, part, edge, ws[k])
+            take, left, right = side_takes(levels, k)
+            edge[pl.ds(0, take), :] = part[pl.ds(left, take), :]
+            edge[pl.ds(take, take), :] = part[pl.ds(2 * w + 16 - right, take), :]
+            count = min(B, levels[k][2])
+            wcs[k][pl.ds(HALO + n * B, count), :] = edge[...].T[:count]
+
+    for d in (0, 1):
         sends[d].wait()
     offsets = stack_offsets(levels)
     for k, a, b, at in rows:
         depth, base = depth_of(levels, k), offsets[k] + 8 * b
         hn[a, pl.ds(base, depth), :] = rows_in[0, pl.ds(at, depth), :]
         hn[a, pl.ds(base + 8 - depth, depth), :] = rows_in[1, pl.ds(at, depth), :]
+    for d in (4, 5, 6, 7):
+        sends[d].wait()
     low, bottom = iota(1) < 64, iota(0) < 4
     for q, (k, a) in enumerate(arrays):
         tile = jnp.where(
@@ -382,9 +451,11 @@
 
 def strip_kernel(levels, *refs):
     ws, zts, ct, image = refs[:4], refs[4:8], refs[8], refs[9]
-    out = refs[10]
-    lows = (None,) + refs[11:14]
-    ends, us, lifted, edge, th, out_sem, end_sem = refs[14:]
+    zs, c4, wcs = refs[10:14], refs[14], refs[15:19]
+    out = refs[19]
+    lows = (None,) + refs[20:23]
+    sides = (None,) + refs[23:26]
+    ends, us, lifted, edge, th, tc, sd, pair, uc, strip, merged, out_sem, end_sem = refs[26:]
     top = len(levels) - 1
     _, blocks, h = levels[top]
     rows = 2 * h
@@ -395,11 +466,17 @@
         return pltpu.make_async_copy(
             image.at[j, pl.ds(HALO + cut, rows - 2 * cut), :], out.at[at, pl.ds(start, B)], out_sem.at[j])
 
+    def flank(side):
+        at = pl.ds(cut, rows - 2 * cut)
+        start = (0, (2 * blocks - 1) * B)[side]
+        return pltpu.make_async_copy(merged.at[side], out.at[at, pl.ds(start, B)],
+                                     out_sem.at[(0, 2 * blocks - 1)[side]])
+
     def send(j, carry):
         main(j, pl.multiple_of(j * B, B)).start()
         return carry
 
-    lax.fori_loop(0, 2 * blocks, send, 0)
+    lax.fori_loop(1, 2 * blocks - 1, send, 0)
 
     for k, level in enumerate(levels):
         _, nb, h = level
@@ -416,6 +493,28 @@
             side = lows[k][nb].T * UP2
             t[pl.ds(0, 8), :] = side[B - 8 :]
             t[pl.ds(HALO + w, 8), :] = side[:8]
+        run = keep // 8
+        take, left, right = side_takes(levels, k)
+        for n in range(row_blocks(level)):
+            if k == 0:
+                side_t, second = c4.at[n], HALO + w + 4 - 8 * run
+            else:
+                tc[n] = sides[k][pl.ds(HALO + n * B, B), :].T * UP2
+                side_t, second = tc.at[n], 8 + 2 * keep + 4 - 8 * run
+            lift_runs(run, side_t, 4, zs[k].at[n], 4, sd.at[n, 0, pl.ds(0, 16 * run), :])
+            lift_runs(run, side_t, second, zs[k].at[n], HALO + w + 4 - 8 * run, sd.at[n, 1, pl.ds(0, 16 * run), :])
+            pair[n, pl.ds(0, take), :] = sd[n, 0, pl.ds(left, take), :]
+            pair[n, pl.ds(take, take), :] = sd[n, 1, pl.ds(16 * run - right, take), :]
+            count = min(B, h)
+            uc[pl.ds(HALO + n * B, count), :] = pair[n].T[:count]
+        lift_rows(h, uc, wcs[k], strip if final else sides[k + 1])
+        if final:
+            low = lax.broadcasted_iota(jnp.int32, (rows - 2 * cut, B), 1) < 64
+            at = pl.ds(HALO + cut, rows - 2 * cut)
+            merged[0] = jnp.where(low, strip[at, :], image[0, at, :])
+            merged[1] = jnp.where(low, image[2 * nb - 1, at, :], strip[at, :])
+            for side in range(2):
+                flank(side).start()
         part = lifted.at[pl.ds(0, 2 * w + 16), :]
         lift_rows(w, t, zts[k], part)
         for j in range(2 * nb):
@@ -458,9 +557,12 @@
 
             lax.fori_loop(0, 2 * nb, body, 0)
             for j in range(2 * nb):
-                main(j, j * B).wait()
+                if 0 < j < 2 * nb - 1:
+                    main(j, j * B).wait()
                 for side in range(2):
                     end(j, side, j * B).wait()
+            for side in range(2):
+                flank(side).wait()
 
 
 def per_device(coarse, d4, d3, d2, d1):
@@ -478,58 +580,69 @@
     strips = [(n, l[2] + 2 * HALO, B) for n, l in zip(wide, levels)]
     stack = (B + 2 * HALO, B)
     blocks, h = levels[top][1], levels[top][2]
+    mb = across[top][0]
     long = 2 * blocks * B + 2 * HALO
-    bands = [(l[1] + 1, l[2] + 2 * HALO, B) for l in levels[1:]]
+    tall = [(l[2] + 2 * HALO, B) for l in levels]
     between = pl.pallas_call(
         functools.partial(exchange_kernel, levels),
         out_shape=[pltpu.VMEM(s, F32) for s in (
-            strips + [s[1:] for s in across] + [across[0][1:], (2 * blocks, 2 * h + 2 * HALO, B)])],
+            strips + [s[1:] for s in across] + [across[0][1:], (2 * blocks, 2 * h + 2 * HALO, B)]
+            + across + [across[0]] + tall)],
         in_specs=[hbm] * 5,
-        out_specs=[vmem] * 10,
+        out_specs=[vmem] * 19,
         scratch_shapes=[
             *[pltpu.VMEM((a, max(B, h), b * B), F32) for a, b, h in levels],
             *[pltpu.VMEM((2,) + s, F32) for s in across],
-            *[pltpu.VMEM(s, F32) for s in across],
-            *[pltpu.VMEM(s, F32) for s in strips],
-            *[pltpu.VMEM(s, F32) for s in bands],
-            *[pltpu.VMEM(s, F32) for s in across],
+            *[pltpu.VMEM((n, 2 * l[1] * B + 2 * HALO, B), F32) for (n, _, _), l in zip(across, levels)],
+            *[pltpu.VMEM(s, F32) for s in strips[:top] + [(1, 8, B)]],
+            *[pltpu.VMEM((l[1], l[2] + 2 * HALO, B), F32) for l in levels[1:]],
+            *[pltpu.VMEM(s, F32) for s in across[1:]],
             pltpu.VMEM((4, B, B), F32),
             pltpu.VMEM((4, B, B), F32),
             pltpu.VMEM(stack, F32),
             pltpu.VMEM(stack, F32),
             pltpu.VMEM((2 * B + 2 * HALO, B), F32),
-            pltpu.VMEM((across[top][0], long, B), F32),
+            pltpu.VMEM((mb, long, B), F32),
             pltpu.VMEM((B, B), F32),
             pltpu.VMEM((1 + sum(l[1] for l in levels), B, B), F32),
+            pltpu.VMEM(tall[top], F32),
+            pltpu.VMEM(tall[top], F32),
             pltpu.VMEM((2, row_count, B), F32),
             pltpu.VMEM((2, col_count, B), F32),
             pltpu.VMEM((4, 8, B), F32),
             pltpu.VMEM((2, row_count, B), F32),
             pltpu.VMEM((2, col_count, B), F32),
             pltpu.VMEM((4, 8, B), F32),
-            pltpu.SemaphoreType.DMA((11,)),
+            pltpu.SemaphoreType.DMA((15,)),
             pltpu.SemaphoreType.DMA((8,)),
             pltpu.SemaphoreType.DMA((8,)),
         ],
         compiler_params=pltpu.CompilerParams(
-            collective_id=0, has_side_effects=True, vmem_limit_bytes=40 * 2**20),
+            collective_id=0, has_side_effects=True, vmem_limit_bytes=41 * 2**20),
     )(*[pltpu.with_memory_space_constraint(x, pltpu.HBM) for x in (coarse, d4, d3, d2, d1)])
     return pl.pallas_call(
         functools.partial(strip_kernel, levels),
         out_shape=jax.ShapeDtypeStruct((2 * h, 2 * blocks * B), F32),
-        in_specs=[vmem] * 10,
+        in_specs=[vmem] * 19,
         out_specs=pl.BlockSpec(memory_space=pl.ANY),
         scratch_shapes=[
             *[pltpu.VMEM((l[1] + 1, B, B), F32) for l in levels[1:]],
+            *[pltpu.VMEM(s, F32) for s in tall[1:]],
             pltpu.VMEM((2, 2 * blocks, 16 * (strip_rows(top) // 8), B), F32),
             pltpu.VMEM((2 * blocks, B, B), F32),
             pltpu.VMEM((long, B), F32),
             pltpu.VMEM((B, B), F32),
             pltpu.VMEM(across[top][1:], F32),
+            pltpu.VMEM((mb, B, B), F32),
+            pltpu.VMEM((mb, 2, 16 * (strip_rows(top) // 8), B), F32),
+            pltpu.VMEM((mb, B, B), F32),
+            pltpu.VMEM(tall[top], F32),
+            pltpu.VMEM((2 * h + 2 * HALO, B), F32),
+            pltpu.VMEM((2, 2 * h - 128, B), F32),
             pltpu.SemaphoreType.DMA((2 * blocks,)),
             pltpu.SemaphoreType.DMA((2, 2 * blocks)),
         ],
-        compiler_params=pltpu.CompilerParams(vmem_limit_bytes=12 * 2**20),
+        compiler_params=pltpu.CompilerParams(vmem_limit_bytes=14 * 2**20),
     )(*between)
 
 

time: 24.2 us -> 20.8 us (0.86)
  the two profiles are of different devices: /device:TPU:0 before, /device:TPU:7 now
where the time goes in v4:
time: 20.8 us; the launch traced here: 20.7 us
  Pallas kernels  20.7 us (100%)
    pallas_call x1, Pallas kernels, per_device(): pl.pallas_call(functools.partial(exchange_kernel, levels), out_shape=[plt...  16.8 us
    pallas_call x1, Pallas kernels, per_device(): pl.pallas_call(functools.partial(strip_kernel, levels), out_shape=jax.Sha...  3.87 us

profile of v4, /device:TPU:7, one launch (start us, length us, event | category | flops | bytes accessed | tf_op | source)
XLA Modules:
  0.0 20.7 jit_solution(11616318644695511681)
XLA Ops:
  0.0 16.8 %shard_map.55 = (f32[3,80,128]{2,1,0:T(8,128)S(1)}, f32[5,144,128]{2,1,0:T(8,128)S(1)}, f32[9,272,128]{2,1,0:T(8,128)S(1)}, f32[16,528,128]{2,1,0:T(8,128)S(1)},...) custom-call(f32[64,128]{1,0:T(8,128)} %refs_0_.1, ...), custom_call_target="tpu_custom_call" | custom-call | tf_op jit(solution)/shard_map/pallas_call | solution.py:586
  16.9 3.9 %shard_map.56 = f32[1024,2048]{1,0:T(8,128)} custom-call(f32[3,80,128]{2,1,0:T(8,128)S(1)} %get-tuple-element.24.refs_0_, f32[5,144,128]{2,1,0:T(8,128)S(1)} %get-tuple-element.25.refs_1_, f32[9,272,128]{2,1,0:T(8,128)S(1)} %get-tuple-element.26.refs_2_, f32[16,528,128]{2,1,0:T(8,128)S(1)} %get-tuple-element.27.refs_3_, ...), custom_call_target="tpu_custom_call" | custom-call | tf_op jit(solution)/shard_map/pallas_call | solution.py:623

commit v5 on v4

--- a/solution.py
+++ b/solution.py
@@ -192,7 +192,7 @@
     zs, c4, wcs = refs[15:19], refs[19], refs[20:24]
     ns, xs, ls, us = refs[24:28], refs[28:32], refs[32:36], refs[36:40]
     lows, ts = (None,) + refs[40:43], (c4,) + refs[43:46]
-    (hn, cn, sh, rh, hd, lifted, edge, ds, even, odd, rows_out, cols_out, corners_out,
+    (hn, cn, sh, rh, hd, lifted, edge, ds, rows_out, cols_out, corners_out,
      rows_in, cols_in, corners_in, load_sem, send_sem, recv_sem) = refs[46:]
     nr, nc = lax.axis_size("rows"), lax.axis_size("cols")
     r, c = lax.axis_index("rows"), lax.axis_index("cols")
@@ -300,19 +300,19 @@
     second = jnp.logical_and(rest, jnp.logical_not(quick))
     pl.when(at_once)(enter)
 
-    for copy in loads[edge_loads:side_loads]:
+    for copy in loads[edge_loads : edge_loads + 2]:
         copy.wait()
-
-    def blocks_of(k, which):
-        blocks = levels[k][1]
-        sides = sorted({0, blocks - 1})
-        return sides if which == "sides" else range(1, blocks - 1)
-
-    for k in range(top + 1):
+    for k in range(top):
         for a in range(levels[k][0]):
             for n in range(row_blocks(levels[k])):
-                for b in blocks_of(k, "sides"):
+                for b in range(levels[k][1]):
                     transpose(k, a, n, b)
+    for copy in loads[edge_loads + 2 : side_loads]:
+        copy.wait()
+    for a in range(3):
+        for n in range(row_blocks(levels[top])):
+            for b in (0, levels[top][1] - 1):
+                transpose(top, a, n, b)
     columns, _ = column_plan(levels)
     for k, a, n, at in columns:
         depth, w = depth_of(levels, k), levels[k][1] * B
@@ -322,67 +322,52 @@
     pl.when(at_once)(enter_sides)
     pl.when(second)(enter_all)
 
-    for k in range(top):
-        for a in range(levels[k][0]):
-            for n in range(row_blocks(levels[k])):
-                for b in blocks_of(k, "middle"):
-                    transpose(k, a, n, b)
-    for copy in loads[side_loads:]:
-        copy.wait()
-
-    def middle(a, carry):
-        for n in range(row_blocks(levels[top])):
-            for b in blocks_of(top, "middle"):
-                at = pl.ds(HALO + b * B, B)
-                block = ns[top][a, pl.ds(n * B, B), pl.ds(b * B, B)].T
-                xs[top][a - 1, n, at, :] = block * jnp.where(a == 2, F32(DOWN2), F32(1.0))
-        return carry
-
-    for n in range(row_blocks(levels[top])):
-        for b in blocks_of(top, "middle"):
-            transpose(top, 0, n, b)
-    lax.fori_loop(1, 3, middle, 0)
-    for k in (3, 2, 1, 0):
+    def details(k):
         for n in range(row_blocks(levels[k])):
             lift_rows(levels[k][1] * B, xs[k].at[0, n], xs[k].at[1, n], ls[k].at[n])
             turn_back(levels[k], n, ls[k].at[n], ws[k], range(2 * levels[k][1]))
 
-    pl.when(third)(enter_all)
-
-    for k, level in enumerate(levels):
-        _, blocks, h = level
-        w = blocks * B
-        n_rows = row_blocks(level)
-        for n in range(n_rows):
+    def inner(k, count, s, r, dst):
+        start = (-4, 4, 12, 28)[k]
+        run = (count - 2 * start) // 8
+        at = HALO + start
+        lift_runs(run, s, at, r, at, dst.at[pl.ds(HALO + 2 * start, 16 * run), :])
+
+    def chain_columns(k):
+        _, blocks, h = levels[k]
+        for n in range(row_blocks(levels[k])):
             if k > 0:
                 for b in range(blocks):
                     ts[k][n, pl.ds(HALO + b * B, B), :] = lows[k][b, pl.ds(HALO + n * B, B), :].T * UP2
-            part = lifted.at[n, pl.ds(0, 2 * w + 16), :]
-            lift_rows(w, ts[k].at[n], zs[k].at[n], part)
-            if k < top:
-                turn_back(level, n, part, us[k], range(2 * blocks))
-        if k < top:
-            for j in range(2 * blocks):
-                lift_rows(h, us[k].at[j], ws[k].at[j], lows[k + 1].at[j])
-        if k == top - 1:
-            pl.when(fourth)(enter_all)
-
-    def fill(j, dst):
-        at = pl.ds(pl.multiple_of(HALO + j * B, 8), B)
+            inner(k, blocks * B, ts[k].at[n], zs[k].at[n], lifted.at[n])
+
+    def chain_rows(k, these):
+        h = levels[k][2]
+        for j in these:
+            for n in range(row_blocks(levels[k])):
+                turn_back(levels[k], n, lifted.at[n], us[k], (j,))
+            inner(k, h, us[k].at[j], ws[k].at[j], image.at[j] if k == top else lows[k + 1].at[j])
+
+    for k in range(top):
+        details(k)
+    for k in range(top - 1):
+        chain_columns(k)
+        chain_rows(k, range(2 * levels[k][1]))
+    for copy in loads[side_loads:]:
+        copy.wait()
+    for a in range(3):
         for n in range(row_blocks(levels[top])):
-            dst[pl.ds(HALO + n * B, B), :] = lifted[n, at, :].T
-
-    def body(i, carry):
-        j = 2 * i
-        _, blocks, h = levels[top]
-        fill(j + 1, odd)
-        lift_rows(h, even, ws[top].at[j], image.at[j])
-        fill(jnp.minimum(j + 2, 2 * blocks - 1), even)
-        lift_rows(h, odd, ws[top].at[j + 1], image.at[j + 1])
-        return carry
-
-    fill(0, even)
-    lax.fori_loop(0, levels[top][1], body, 0)
+            for b in range(1, levels[top][1] - 1):
+                transpose(top, a, n, b)
+    chain_columns(top - 1)
+    chain_rows(top - 1, range(2 * levels[top - 1][1]))
+    pl.when(third)(enter_all)
+
+    details(top)
+    chain_columns(top)
+    blocks = levels[top][1]
+    chain_rows(top, range(1, blocks))
+    pl.when(fourth)(enter_all)
 
     for k, (_, blocks, h) in enumerate(levels):
         keep = strip_rows(k)
@@ -413,6 +398,8 @@
             edge[pl.ds(take, take), :] = part[pl.ds(2 * w + 16 - right, take), :]
             count = min(B, levels[k][2])
             wcs[k][pl.ds(HALO + n * B, count), :] = edge[...].T[:count]
+
+    chain_rows(top, (*range(levels[top][1], 2 * levels[top][1]), 0))
 
     for d in (0, 1):
         sends[d].wait()
@@ -594,7 +581,7 @@
             *[pltpu.VMEM((a, max(B, h), b * B), F32) for a, b, h in levels],
             *[pltpu.VMEM((2,) + s, F32) for s in across],
             *[pltpu.VMEM((n, 2 * l[1] * B + 2 * HALO, B), F32) for (n, _, _), l in zip(across, levels)],
-            *[pltpu.VMEM(s, F32) for s in strips[:top] + [(1, 8, B)]],
+            *[pltpu.VMEM(s, F32) for s in strips],
             *[pltpu.VMEM((l[1], l[2] + 2 * HALO, B), F32) for l in levels[1:]],
             *[pltpu.VMEM(s, F32) for s in across[1:]],
             pltpu.VMEM((4, B, B), F32),
@@ -605,8 +592,6 @@
             pltpu.VMEM((mb, long, B), F32),
             pltpu.VMEM((B, B), F32),
             pltpu.VMEM((1 + sum(l[1] for l in levels), B, B), F32),
-            pltpu.VMEM(tall[top], F32),
-            pltpu.VMEM(tall[top], F32),
             pltpu.VMEM((2, row_count, B), F32),
             pltpu.VMEM((2, col_count, B), F32),
             pltpu.VMEM((4, 8, B), F32),

time: 20.8 us -> 19 us (0.913)
  the two profiles are of different devices: /device:TPU:7 before, /device:TPU:1 now
where the time goes in v5:
time: 19 us; the launch traced here: 18.9 us
  Pallas kernels  18.9 us (99%)
    pallas_call x1, Pallas kernels, per_device(): pl.pallas_call(functools.partial(exchange_kernel, levels), out_shape=[plt...  15 us
    pallas_call x1, Pallas kernels, per_device(): pl.pallas_call(functools.partial(strip_kernel, levels), out_shape=jax.Sha...  3.87 us

profile of v5, /device:TPU:1, one launch (start us, length us, event | category | flops | bytes accessed | tf_op | source)
XLA Modules:
  0.0 18.9 jit_solution(11093891846298074380)
XLA Ops:
  0.0 15.0 %shard_map.55 = (f32[3,80,128]{2,1,0:T(8,128)S(1)}, f32[5,144,128]{2,1,0:T(8,128)S(1)}, f32[9,272,128]{2,1,0:T(8,128)S(1)}, f32[16,528,128]{2,1,0:T(8,128)S(1)},...) custom-call(f32[64,128]{1,0:T(8,128)} %refs_0_.1, ...), custom_call_target="tpu_custom_call" | custom-call | tf_op jit(solution)/shard_map/pallas_call | solution.py:573
  15.0 3.9 %shard_map.56 = f32[1024,2048]{1,0:T(8,128)} custom-call(f32[3,80,128]{2,1,0:T(8,128)S(1)} %get-tuple-element.24.refs_0_, f32[5,144,128]{2,1,0:T(8,128)S(1)} %get-tuple-element.25.refs_1_, f32[9,272,128]{2,1,0:T(8,128)S(1)} %get-tuple-element.26.refs_2_, f32[16,528,128]{2,1,0:T(8,128)S(1)} %get-tuple-element.27.refs_3_, ...), custom_call_target="tpu_custom_call" | custom-call | tf_op jit(solution)/shard_map/pallas_call | solution.py:608

commit v6 on v5

--- a/solution.py
+++ b/solution.py
@@ -289,15 +289,24 @@
         enter()
         enter_sides()
 
-    first_row = r < 1
-    fourth = jnp.logical_and(first_row, c < 2)
-    third = jnp.logical_or(
-        jnp.logical_and(first_row, c >= 2),
-        jnp.logical_and(jnp.logical_and(lax.rem(r, 4) < 1, r >= 1), c < 1))
-    rest = jnp.logical_not(jnp.logical_or(third, fourth))
-    quick = jnp.logical_or(jnp.logical_and(c >= 2, lax.rem(c, 2) < 1), c >= nc - 1)
-    at_once = jnp.logical_and(rest, quick)
-    second = jnp.logical_and(rest, jnp.logical_not(quick))
+    def every(*conditions):
+        return functools.reduce(jnp.logical_and, conditions)
+
+    def some(*conditions):
+        return functools.reduce(jnp.logical_or, conditions)
+
+    turned, near, odd = lax.rem(r, 4) < 1, c < 2, lax.rem(c, 2) >= 1
+    first_row, last_row, last_column = r < 1, r >= nr - 1, c >= nc - 1
+    straight, far, even = lax.rem(r, 4) >= 1, c >= 2, lax.rem(c, 2) < 1
+    later_row, inner_row, inner_column = r >= 1, r < nr - 1, c < nc - 1
+    fifth = every(first_row, near)
+    fourth = some(
+        every(first_row, far), every(later_row, turned, near),
+        every(later_row, turned, odd, inner_column, far), every(straight, near, even, inner_row))
+    third = some(
+        every(later_row, turned, far, some(even, last_column)), every(straight, near, odd, inner_row))
+    at_once = every(straight, far, some(even, last_column))
+    second = jnp.logical_not(some(at_once, third, fourth, fifth))
     pl.when(at_once)(enter)
 
     for copy in loads[edge_loads : edge_loads + 2]:
@@ -353,6 +362,7 @@
     for k in range(top - 1):
         chain_columns(k)
         chain_rows(k, range(2 * levels[k][1]))
+    pl.when(third)(enter_all)
     for copy in loads[side_loads:]:
         copy.wait()
     for a in range(3):
@@ -361,13 +371,13 @@
                 transpose(top, a, n, b)
     chain_columns(top - 1)
     chain_rows(top - 1, range(2 * levels[top - 1][1]))
-    pl.when(third)(enter_all)
+    pl.when(fourth)(enter_all)
 
     details(top)
     chain_columns(top)
     blocks = levels[top][1]
     chain_rows(top, range(1, blocks))
-    pl.when(fourth)(enter_all)
+    pl.when(fifth)(enter_all)
 
     for k, (_, blocks, h) in enumerate(levels):
         keep = strip_rows(k)

time: 19 us -> 19 us (level)
  no operation moved by 1% of the time
where the time goes in v6:
time: 19 us; the launch traced here: 18.9 us
  Pallas kernels  18.9 us (99%)
    pallas_call x1, Pallas kernels, per_device(): pl.pallas_call(functools.partial(exchange_kernel, levels), out_shape=[plt...  15 us
    pallas_call x1, Pallas kernels, per_device(): pl.pallas_call(functools.partial(strip_kernel, levels), out_shape=jax.Sha...  3.87 us

profile of v6, /device:TPU:1, one launch (start us, length us, event | category | flops | bytes accessed | tf_op | source)
XLA Modules:
  0.0 18.9 jit_solution(16995191243252915995)
XLA Ops:
  0.0 15.0 %shard_map.55 = (f32[3,80,128]{2,1,0:T(8,128)S(1)}, f32[5,144,128]{2,1,0:T(8,128)S(1)}, f32[9,272,128]{2,1,0:T(8,128)S(1)}, f32[16,528,128]{2,1,0:T(8,128)S(1)},...) custom-call(f32[64,128]{1,0:T(8,128)} %refs_0_.1, ...), custom_call_target="tpu_custom_call" | custom-call | tf_op jit(solution)/shard_map/pallas_call | solution.py:583
  15.0 3.9 %shard_map.56 = f32[1024,2048]{1,0:T(8,128)} custom-call(f32[3,80,128]{2,1,0:T(8,128)S(1)} %get-tuple-element.24.refs_0_, f32[5,144,128]{2,1,0:T(8,128)S(1)} %get-tuple-element.25.refs_1_, f32[9,272,128]{2,1,0:T(8,128)S(1)} %get-tuple-element.26.refs_2_, f32[16,528,128]{2,1,0:T(8,128)S(1)} %get-tuple-element.27.refs_3_, ...), custom_call_target="tpu_custom_call" | custom-call | tf_op jit(solution)/shard_map/pallas_call | solution.py:618

commit v7 on v6

--- a/solution.py
+++ b/solution.py
@@ -40,13 +40,21 @@
     return 2 if k == len(levels) - 1 else 4
 
 
-def row_plan(levels):
+def row_depth(levels, k, a, d):
+    back = len(levels) - 1 - k
+    if d == 0:
+        return (2, 3, 4, 4)[back]
+    return (1, 2, 2, 2)[back] if a in (0, 3) else (2, 3, 3, 3)[back]
+
+
+def row_plan(levels, d):
     plan, at = [], 0
     for k, (arrays, blocks, h) in enumerate(levels):
         for a in range(arrays):
             for b in range(blocks):
-                plan.append((k, a, b, at))
-                at += depth_of(levels, k)
+                depth = row_depth(levels, k, a, d)
+                plan.append((k, a, b, at, depth))
+                at += depth
     return plan, -(-at // 8) * 8
 
 
@@ -243,12 +251,10 @@
 
     for copy in loads[:edge_loads]:
         copy.wait()
-    rows, _ = row_plan(levels)
-    for k, a, b, at in rows:
-        depth, h = depth_of(levels, k), levels[k][2]
-        here = pl.ds(b * B, B)
-        rows_out[0, pl.ds(at, depth), :] = ns[k][a, pl.ds(0, depth), here]
-        rows_out[1, pl.ds(at, depth), :] = ns[k][a, pl.ds(h - depth, depth), here]
+    for d in range(2):
+        for k, a, b, at, depth in row_plan(levels, d)[0]:
+            first = 0 if d == 0 else levels[k][2] - depth
+            rows_out[d, pl.ds(at, depth), :] = ns[k][a, pl.ds(first, depth), pl.ds(b * B, B)]
     group = iota(1) // 4
     arrays = [(k, a) for k in range(top + 1) for a in range(levels[k][0])]
     for d in range(4):
@@ -267,7 +273,8 @@
     sends = []
     for d, step in enumerate(DIRS):
         if d < 2:
-            src, dst = rows_out.at[d], rows_in.at[d]
+            sent = pl.ds(0, row_plan(levels, d)[1])
+            src, dst = rows_out.at[d, sent, :], rows_in.at[d, sent, :]
         elif d < 4:
             src, dst = cols_out.at[d - 2], cols_in.at[d - 2]
         else:
@@ -414,10 +421,15 @@
     for d in (0, 1):
         sends[d].wait()
     offsets = stack_offsets(levels)
-    for k, a, b, at in rows:
-        depth, base = depth_of(levels, k), offsets[k] + 8 * b
-        hn[a, pl.ds(base, depth), :] = rows_in[0, pl.ds(at, depth), :]
-        hn[a, pl.ds(base + 8 - depth, depth), :] = rows_in[1, pl.ds(at, depth), :]
+    for d in range(2):
+        for k, a, b, at, depth in row_plan(levels, d)[0]:
+            incoming = rows_in[d, pl.ds(at, depth), :]
+            if a in (0, 3):
+                first = 8 + 2 * strip_rows(k) if d == 0 else 8 - depth
+                ds[at_of(levels, k, a, b), pl.ds(first, depth), :] = incoming
+            else:
+                first = offsets[k] + 8 * b + (0 if d == 0 else 8 - depth)
+                hn[a, pl.ds(first, depth), :] = incoming
     for d in (4, 5, 6, 7):
         sends[d].wait()
     low, bottom = iota(1) < 64, iota(0) < 4
@@ -430,14 +442,11 @@
         cn[a, pl.ds(offsets[k] + 8 * (levels[k][1] - 1), 8), :] = tile
     halo_transpose(levels, hn.at[1], cn.at[1], None, sh)
     halo_transpose(levels, hn.at[2], cn.at[2], DOWN2, rh)
-    for k, a, b, at in rows:
-        if a in (0, 3):
-            depth, keep = depth_of(levels, k), strip_rows(k)
-            strip = at_of(levels, k, a, b)
-            ds[strip, pl.ds(8 + 2 * keep, depth), :] = rows_in[0, pl.ds(at, depth), :]
-            ds[strip, pl.ds(8 - depth, depth), :] = rows_in[1, pl.ds(at, depth), :]
-            (ct_out if a == 3 else zts[k])[pl.ds(HALO + b * B, B), :] = scaled(
-                ds[strip].T, UP2 if a == 3 else None)
+    for k in range(top + 1):
+        for a in (0, 3) if k == 0 else (0,):
+            for b in range(levels[k][1]):
+                (ct_out if a == 3 else zts[k])[pl.ds(HALO + b * B, B), :] = scaled(
+                    ds[at_of(levels, k, a, b)].T, UP2 if a == 3 else None)
     side = cn[0].T
     for k in range(top + 1):
         strip_sides(levels, k, zs[k], side, zts[k])
@@ -568,7 +577,7 @@
         levels.append((4 if k == 0 else 3, x.shape[2] // B, x.shape[1]))
     levels = tuple(levels)
     top = len(levels) - 1
-    _, row_count = row_plan(levels)
+    row_count = max(row_plan(levels, d)[1] for d in range(2))
     _, col_count = column_plan(levels)
     hbm = pl.BlockSpec(memory_space=pltpu.HBM)
     vmem = pl.BlockSpec(memory_space=pltpu.VMEM)

time: 19 us -> 19 us (level)
  no operation moved by 1% of the time
where the time goes in v7:
time: 19 us; the launch traced here: 18.9 us
  Pallas kernels  18.9 us (99%)
    pallas_call x1, Pallas kernels, per_device(): pl.pallas_call(functools.partial(exchange_kernel, levels), out_shape=[plt...  15 us
    pallas_call x1, Pallas kernels, per_device(): pl.pallas_call(functools.partial(strip_kernel, levels), out_shape=jax.Sha...  3.87 us

profile of v7, /device:TPU:1, one launch (start us, length us, event | category | flops | bytes accessed | tf_op | source)
XLA Modules:
  0.0 18.9 jit_solution(2306204173400335225)
XLA Ops:
  0.0 15.0 %shard_map.55 = (f32[3,80,128]{2,1,0:T(8,128)S(1)}, f32[5,144,128]{2,1,0:T(8,128)S(1)}, f32[9,272,128]{2,1,0:T(8,128)S(1)}, f32[16,528,128]{2,1,0:T(8,128)S(1)},...) custom-call(f32[64,128]{1,0:T(8,128)} %refs_0_.1, ...), custom_call_target="tpu_custom_call" | custom-call | tf_op jit(solution)/shard_map/pallas_call | solution.py:592
  15.1 3.9 %shard_map.56 = f32[1024,2048]{1,0:T(8,128)} custom-call(f32[3,80,128]{2,1,0:T(8,128)S(1)} %get-tuple-element.24.refs_0_, f32[5,144,128]{2,1,0:T(8,128)S(1)} %get-tuple-element.25.refs_1_, f32[9,272,128]{2,1,0:T(8,128)S(1)} %get-tuple-element.26.refs_2_, f32[16,528,128]{2,1,0:T(8,128)S(1)} %get-tuple-element.27.refs_3_, ...), custom_call_target="tpu_custom_call" | custom-call | tf_op jit(solution)/shard_map/pallas_call | solution.py:627
